TPU v7x, 32 devices: a whole 2x2x4 slice. The times are simulated.
32 devices in a mesh: row: 4 (over z), col: 8 (over y, x, core).
Axes of the slice: x: 2, y: 2, z: 4, core: 2. Of those that a mesh axis runs over, the one named last changes fastest.
Arguments:
- right_side: float32 [256, 2048], P('row', 'col'), may hold values from -20 to 20
- initial_guess: float32 [256, 2048], P('row', 'col'), may hold values from -3 to 3
- kernel: float32 [31, 31], replicated, may hold values from 0 to 1, as said below
Outputs:
- template: float32 [256, 2048], P('row', 'col')
- residual: float32 [256, 2048], P('row', 'col')
Inputs may be any that keep to these rules, and one draw needn't show every extreme that they name: `kernel`: entries are positive and sum to one.
All inputs are finite; a program needn't handle non-finite values.
Results may differ from a plain program's by a relative error of at most 0.0003.
Values sent between devices are 32-bit elements; how exact they have to be, the bound alone decides.
A program may use at most 128 MiB of HBM per device.

v0:
```python
import functools

import jax
import jax.numpy as jnp
from jax import lax
from jax.experimental import pallas as pl
from jax.experimental.pallas import tpu as pltpu
from jax.sharding import PartitionSpec as P

ITERS = 3
PENALTY = 0.05
EDGE_ROWS = 16
EDGE_COLS = 128
DEPTH = 512
LANES = 128
MESH = pl.DeviceIdType.MESH
DIRECTIONS = ((-1, -1), (-1, 1), (1, -1), (1, 1), (0, -1), (0, 1), (-1, 0), (1, 0))
SIDES = (4, 5)
OTHERS = (0, 1, 2, 3, 6, 7)


def span(step, size, edge):
    if step > 0:
        return size, 0, edge
    if step < 0:
        return edge, size + edge, edge
    return edge, edge, size


def split(x):
    high = x.astype(jnp.bfloat16)
    low = (x - high.astype(jnp.float32)).astype(jnp.bfloat16)
    return high, low


def body(
    n_row, n_col,
    right_ref, guess_ref, kernel_ref, template_ref, residual_ref,
    ext, taps_ref, mid_table, edge_table, got, smooth_ref, along_ref, direction_ref, last_ref,
    red, send_sem, recv_sem, red_send, red_recv,
):
    rows, cols = right_ref.shape
    row, col = lax.axis_index("row"), lax.axis_index("col")
    me, count = row * n_col + col, n_row * n_col
    tall, wide = rows + 2 * EDGE_ROWS, cols + 2 * EDGE_COLS
    width = kernel_ref.shape[0]
    half = width // 2
    shifts = mid_table.shape[1] * LANES // rows
    mid_r, mid_c = pl.ds(EDGE_ROWS, rows), pl.ds(EDGE_COLS, cols)

    barrier = pltpu.get_barrier_semaphore()

    def others(act):
        def along_row(r, carry):
            def one(c, inner):
                pl.when(r * n_col + c != me)(lambda: act((r, c)))
                return inner

            return lax.fori_loop(0, n_col, one, carry)

        lax.fori_loop(0, n_row, along_row, 0)

    others(
        lambda place: pl.semaphore_signal(barrier, inc=1, device_id=place, device_id_type=MESH)
    )

    phases = ext.shape[0]
    ext[0, mid_r, mid_c] = guess_ref[...]

    @pl.when(row == 0)
    def _():
        ext[:, 0:EDGE_ROWS, :] = jnp.zeros((phases, EDGE_ROWS, wide), jnp.float32)

    @pl.when(row == n_row - 1)
    def _():
        ext[:, EDGE_ROWS + rows : tall, :] = jnp.zeros((phases, EDGE_ROWS, wide), jnp.float32)

    @pl.when(col == 0)
    def _():
        ext[:, :, 0:EDGE_COLS] = jnp.zeros((phases, tall, EDGE_COLS), jnp.float32)

    @pl.when(col == n_col - 1)
    def _():
        ext[:, :, EDGE_COLS + cols : wide] = jnp.zeros((phases, tall, EDGE_COLS), jnp.float32)

    def inside(dr, dc):
        checks = []
        if dr:
            checks.append(row + dr >= 0 if dr < 0 else row + dr < n_row)
        if dc:
            checks.append(col + dc >= 0 if dc < 0 else col + dc < n_col)
        return functools.reduce(jnp.logical_and, checks)

    def strip(phase, index):
        dr, dc = DIRECTIONS[index]
        r_src, r_dst, r_len = span(dr, rows, EDGE_ROWS)
        c_src, c_dst, c_len = span(dc, cols, EDGE_COLS)
        return pltpu.make_async_remote_copy(
            src_ref=ext.at[phase, pl.ds(r_src, r_len), pl.ds(c_src, c_len)],
            dst_ref=ext.at[phase, pl.ds(r_dst, r_len), pl.ds(c_dst, c_len)],
            send_sem=send_sem.at[phase, index],
            recv_sem=recv_sem.at[phase, index],
            device_id=(row + dr, col + dc),
            device_id_type=MESH,
        )

    def send(phase):
        for index, (dr, dc) in enumerate(DIRECTIONS):
            pl.when(inside(dr, dc))(lambda index=index: strip(phase, index).start())

    def receive(phase, which):
        for index in which:
            dr, dc = DIRECTIONS[index]
            pl.when(inside(-dr, -dc))(lambda index=index: strip(phase, index).wait_recv())

    def finish(phase):
        for index, (dr, dc) in enumerate(DIRECTIONS):
            pl.when(inside(dr, dc))(lambda index=index: strip(phase, index).wait_send())

    sub = lax.broadcasted_iota(jnp.int32, (8, LANES), 0)
    lane8 = lax.broadcasted_iota(jnp.int32, (8, LANES), 1)
    per_mid, edge_span = LANES // rows, 2 * EDGE_ROWS
    per_edge = LANES // edge_span

    def flip(x):
        return jnp.concatenate([x[a : a + 1] for a in reversed(range(width))] + [x[width:]], axis=0)

    def prepare():
        taps = kernel_ref[...]
        taps = jnp.concatenate([taps, jnp.zeros((width, LANES - width), jnp.float32)], axis=1)
        taps = jnp.concatenate([taps, jnp.zeros((LANES - width, LANES), jnp.float32)], axis=0)
        taps_ref[0] = taps.T
        taps_ref[1] = flip(flip(taps).T)

    def build(which, quad):
        bands = []
        for q in range(per_edge):
            line = taps_ref[which, pl.ds(quad * per_edge + q, 1), :]
            eight = pltpu.roll(jnp.broadcast_to(line, (8, LANES)), EDGE_ROWS - half, axis=1)
            for bit in (1, 2, 4):
                eight = jnp.where((sub & bit) != 0, pltpu.roll(eight, bit, axis=1), eight)
            bands.append(eight)

        def moved(q, k, shift):
            return pltpu.roll(bands[q], (8 * k + shift) % LANES, axis=1)

        def keep(table, tile, blocks):
            high, low = split(jnp.concatenate(blocks, axis=0))
            table[which, tile, 0:rows, :] = high
            table[which, tile, rows : 2 * rows, :] = low

        for t in range(per_edge // per_mid):
            blocks = []
            for k in range(rows // 8):
                block = moved(t * per_mid, k, -EDGE_ROWS)
                for q in range(1, per_mid):
                    other = moved(t * per_mid + q, k, q * rows - EDGE_ROWS)
                    block = jnp.where(lane8 < q * rows, block, other)
                blocks.append(block)
            keep(mid_table, quad * (per_edge // per_mid) + t, blocks)
        blocks = []
        for k in range(rows // 8):
            block = None
            for q in range(per_edge):
                start = q * edge_span
                upper = moved(q, k, start)
                lower = moved(q, k, start - rows)
                piece = jnp.where(lane8 < start + EDGE_ROWS, upper, lower)
                block = piece if block is None else jnp.where(lane8 < start, block, piece)
            blocks.append(block)
        keep(edge_table, quad, blocks)

    def build_half(which):
        def inner(quad, c):
            build(which, quad)
            return c

        lax.fori_loop(0, shifts // per_edge, inner, 0)

    def part(source, table, which):
        depth = source.shape[0]
        group = DEPTH // depth
        both = jnp.zeros((2 * rows, cols), jnp.float32)
        rest = jnp.zeros((rows, cols), jnp.float32)
        for first in range(0, shifts, group):
            highs, lows = [], []
            for b in range(first, first + group):
                offset = EDGE_COLS - half + min(b, width - 1)
                high, low = split(pltpu.roll(source, wide - offset, axis=1)[:, 0:cols])
                highs.append(high)
                lows.append(low)
            tiles = range(first * depth // LANES, (first + group) * depth // LANES)
            block = jnp.concatenate([table[which, t] for t in tiles], axis=1)
            both = both + jnp.dot(
                block, jnp.concatenate(highs, axis=0), preferred_element_type=jnp.float32
            )
            rest = rest + jnp.dot(
                block[0:rows], jnp.concatenate(lows, axis=0), preferred_element_type=jnp.float32
            )
        return both[0:rows] + (both[rows:] + rest)

    def correlate(phase, which):
        receive(phase, SIDES)
        middle = part(ext[phase, mid_r, :], mid_table, which)
        receive(phase, OTHERS)
        edges = jnp.concatenate(
            [ext[phase, 0:EDGE_ROWS, :], ext[phase, EDGE_ROWS + rows : tall, :]], axis=0
        )
        return middle + part(edges, edge_table, which)

    def laplacian(phase):
        center = ext[phase, mid_r, mid_c]
        upper = ext[phase, pl.ds(EDGE_ROWS - 1, rows), mid_c]
        lower = ext[phase, pl.ds(EDGE_ROWS + 1, rows), mid_c]
        band = ext[phase, mid_r, :]
        left = pltpu.roll(band, 1, axis=1)[:, EDGE_COLS : EDGE_COLS + cols]
        right = pltpu.roll(band, wide - 1, axis=1)[:, EDGE_COLS : EDGE_COLS + cols]
        return 4.0 * center - upper - lower - left - right

    def put(phase, value):
        ext[phase, mid_r, mid_c] = value
        send(phase)

    lane = lane8[0:1]

    def fold(x):
        line = jnp.sum(x, axis=0, keepdims=True)
        line = functools.reduce(
            jnp.add, [line[:, k : k + 128] for k in range(0, line.shape[1], 128)]
        )
        return line + pltpu.roll(line, 64, axis=1)

    def spread(slot, norms, products):
        red[slot, me] = jnp.where(lane < 64, fold(norms), fold(products))
        others(
            lambda place: pltpu.make_async_remote_copy(
                src_ref=red.at[slot, me],
                dst_ref=red.at[slot, me],
                send_sem=red_send.at[slot],
                recv_sem=red_recv.at[slot],
                device_id=place,
                device_id_type=MESH,
            ).start()
        )

    def all_slots(slot):
        return pltpu.make_async_remote_copy(
            src_ref=red.at[slot, pl.ds(0, count - 1)],
            dst_ref=red.at[slot, pl.ds(0, count - 1)],
            send_sem=red_send.at[slot],
            recv_sem=red_recv.at[slot],
            device_id=(row, col),
            device_id_type=MESH,
        )

    def gather(slot):
        all_slots(slot).wait_recv()
        line = jnp.sum(red[slot], axis=0)
        norm = jnp.sum(jnp.where(lane < 64, line, 0.0), axis=1, keepdims=True)
        product = jnp.sum(jnp.where(lane < 64, 0.0, line), axis=1, keepdims=True)
        return norm, product

    template_ref[...] = guess_ref[...]
    along_ref[...] = jnp.zeros_like(along_ref)
    direction_ref[...] = jnp.zeros_like(direction_ref)
    last_ref[...] = jnp.ones_like(last_ref)
    prepare()
    build_half(0)
    pl.semaphore_wait(barrier, count - 1)
    send(0)
    build_half(1)

    def update(slot):
        applied = got[...] + smooth_ref[...]
        residual = residual_ref[...]
        norm, product = gather(slot)
        norm_last, step_last = last_ref[0:1, 0:1], last_ref[1:2, 0:1]
        ratio = jnp.where(slot > 0, norm / norm_last, 0.0)
        step_size = norm / (product - ratio * norm / step_last)
        direction = residual + ratio * direction_ref[...]
        along = applied + ratio * along_ref[...]
        direction_ref[...], along_ref[...] = direction, along
        last_ref[0:1, :] = jnp.broadcast_to(norm, (1, LANES))
        last_ref[1:2, :] = jnp.broadcast_to(step_size, (1, LANES))
        template_ref[...] = template_ref[...] + step_size * direction
        residual_ref[...] = residual - step_size * along

    def advance(phase, carry):
        which, slot = lax.rem(phase, 2), phase // 2 - 1
        got[...] = correlate(phase, which)

        @pl.when(which == 0)
        def _():
            put(phase + 1, got[...])
            smooth = PENALTY * laplacian(phase)
            smooth_ref[...] = smooth

            @pl.when(slot >= 0)
            def _():
                blurred, center = got[...], ext[phase, mid_r, mid_c]
                spread(slot, center * center, blurred * blurred + center * smooth_ref[...])

        @pl.when(which == 1)
        def _():
            @pl.when(slot < 0)
            def _():
                residual_ref[...] = right_ref[...] - (got[...] + smooth_ref[...])

            @pl.when(slot >= 0)
            def _():
                update(slot)

            @pl.when(phase < phases - 1)
            def _():
                put(phase + 1, residual_ref[...])

            @pl.when(slot >= 0)
            def _():
                all_slots(slot).wait_send()

        finish(phase)
        return carry

    lax.fori_loop(0, phases, advance, 0)


def on_device(n_row, n_col, right_side, initial_guess, kernel):
    rows, cols = right_side.shape
    tall = rows + 2 * EDGE_ROWS
    group = DEPTH // (2 * EDGE_ROWS)
    shifts = -(-kernel.shape[0] // group) * group
    phases, count = 2 * (ITERS + 1), n_row * n_col
    shape = jax.ShapeDtypeStruct((rows, cols), jnp.float32)
    vmem = pl.BlockSpec(memory_space=pltpu.VMEM)
    return pl.pallas_call(
        functools.partial(body, n_row, n_col),
        out_shape=(shape, shape),
        in_specs=[vmem] * 3,
        out_specs=(vmem, vmem),
        scratch_shapes=[
            pltpu.VMEM((phases, tall, cols + 2 * EDGE_COLS), jnp.float32),
            pltpu.VMEM((2, LANES, LANES), jnp.float32),
            pltpu.VMEM((2, shifts * rows // LANES, 2 * rows, LANES), jnp.bfloat16),
            pltpu.VMEM((2, shifts * 2 * EDGE_ROWS // LANES, 2 * rows, LANES), jnp.bfloat16),
            pltpu.VMEM((rows, cols), jnp.float32),
            pltpu.VMEM((rows, cols), jnp.float32),
            pltpu.VMEM((rows, cols), jnp.float32),
            pltpu.VMEM((rows, cols), jnp.float32),
            pltpu.VMEM((8, LANES), jnp.float32),
            pltpu.VMEM((ITERS, count, 1, 128), jnp.float32),
            pltpu.SemaphoreType.DMA((phases, len(DIRECTIONS))),
            pltpu.SemaphoreType.DMA((phases, len(DIRECTIONS))),
            pltpu.SemaphoreType.DMA((ITERS,)),
            pltpu.SemaphoreType.DMA((ITERS,)),
        ],
        compiler_params=pltpu.CompilerParams(collective_id=0, has_side_effects=True),
    )(right_side, initial_guess, kernel)


def solution(mesh):
    placed = (P("row", "col"), P("row", "col"), P())
    return jax.shard_map(
        functools.partial(on_device, mesh.shape["row"], mesh.shape["col"]),
        mesh=mesh,
        in_specs=placed,
        out_specs=(P("row", "col"), P("row", "col")),
        check_vma=False,
    )
```

profile of v0, /device:TPU:0, one launch (start us, length us, event | category | flops | bytes accessed | tf_op | source)
XLA Modules:
  0.0 51.3 jit_solution(3740846913071587024)
XLA Ops:
  0.6 48.5 %shard_map.50 = (f32[64,256]{1,0:T(8,128)}, f32[64,256]{1,0:T(8,128)}) custom-call(f32[64,256]{1,0:T(8,128)} %right_ref.1, f32[64,256]{1,0:T(8,128)} %guess_ref.1, f32[31,31]{1,0:T(8,128)} %kernel_ref.1), custom_call_target="tpu_custom_call" | custom-call | tf_op jit(solution)/shard_map/pallas_call | solution.py:335
  49.2 0.0 copy-start
  49.2 1.5 %copy.7 = f32[64,256]{1,0:T(8,128)} copy(f32[64,256]{1,0:T(8,128)} %get-tuple-element.4) | data formatting | bytes 131072
  50.7 0.0 copy-done
  50.7 0.6 %copy.8 = f32[64,256]{1,0:T(8,128)} copy(f32[64,256]{1,0:T(8,128)S(1)} %copy-done) | data formatting | bytes 131072
Async XLA Ops:
  49.2 1.5 %copy-start = (f32[64,256]{1,0:T(8,128)S(1)}, f32[64,256]{1,0:T(8,128)}, u32[]{:S(2)}) copy-start(f32[64,256]{1,0:T(8,128)} %get-tuple-element.5) | copy-start | bytes 196612
where the time goes:
time: 51.5 us; the launch traced here: 51.3 us
  Pallas kernels  48.5 us (94%)
  local copies, waits for them, and re-layouts  2.14 us (4%)
  between operations  0.65 us (1%)
    pallas_call x1, Pallas kernels, on_device(): pl.pallas_call(functools.partial(body, n_row, n_col), out_shape=(shape, s...  48.5 us
    unnamed x4, local copies, waits for them, and re-layouts  2.14 us

commit v1 on v0

v1 whole, which is shorter than its diff:
```python
import functools

import jax
import jax.numpy as jnp
from jax import lax
from jax.experimental import pallas as pl
from jax.experimental.pallas import tpu as pltpu
from jax.sharding import PartitionSpec as P

PENALTY = 0.05
LANES = 128
MESH = pl.DeviceIdType.MESH
DIRECTIONS = ((-1, 0), (1, 0), (-1, -1), (-1, 1), (1, -1), (1, 1), (0, -1), (0, 1))
MOMENTS = 6


def split(x):
    high = x.astype(jnp.bfloat16)
    low = (x - high.astype(jnp.float32)).astype(jnp.bfloat16)
    return high, low


def body(
    n_row, n_col,
    right_hbm, guess_hbm, kernel_hbm, template_ref, residual_ref,
    right_ref, guess_ref, kernel_ref, packed, packed_right, lines_ref, table, high_ref, low_ref,
    wide0, wide1, partial_ref, block_ref, state_ref, basis_ref, red,
    load_sem, send_sem, recv_sem, red_send, red_recv,
):
    rows, cols = right_ref.shape
    row, col = lax.axis_index("row"), lax.axis_index("col")
    me, count = row * n_col + col, n_row * n_col
    width = kernel_ref.shape[0]
    blk = rows // 2
    edge = rows
    total = cols + 2 * edge
    groups, own_g, edge_g = total // 16, cols // 16, edge // 16

    barrier = pltpu.get_barrier_semaphore()

    def others(act):
        def along_row(r, carry):
            def one(c, inner):
                pl.when(r * n_col + c != me)(lambda: act((r, c)))
                return inner

            return lax.fori_loop(0, n_col, one, carry)

        lax.fori_loop(0, n_row, along_row, 0)

    others(
        lambda place: pl.semaphore_signal(barrier, inc=1, device_id=place, device_id_type=MESH)
    )
    loads = [
        pltpu.make_async_copy(src, dst, load_sem.at[k])
        for k, (src, dst) in enumerate(
            ((kernel_hbm, kernel_ref), (guess_hbm, guess_ref), (right_hbm, right_ref))
        )
    ]
    for load in loads:
        load.start()

    lane = lax.broadcasted_iota(jnp.int32, (8, LANES), 1)
    lane1 = lane[0:1]

    def low_half(shape):
        return lax.broadcasted_iota(jnp.int32, shape, len(shape) - 1) < LANES // 2

    def quarters(a, b, c, d):
        q = lax.broadcasted_iota(jnp.int32, a.shape, 1)
        return jnp.where(
            q < 2 * blk, jnp.where(q < blk, a, b), jnp.where(q < 3 * blk, c, d)
        )

    def inside(dr, dc):
        checks = []
        if dr:
            checks.append(row + dr >= 0 if dr < 0 else row + dr < n_row)
        if dc:
            checks.append(col + dc >= 0 if dc < 0 else col + dc < n_col)
        return functools.reduce(jnp.logical_and, checks)

    def clear(buf, lead):
        zero_tall = jnp.zeros(lead + (1, groups, 8, LANES), jnp.float32)
        zero_edge = jnp.zeros(lead + (3, edge_g, 8, LANES), jnp.float32)
        at = (slice(None),) * len(lead)

        @pl.when(row == 0)
        def _():
            buf[at + (slice(0, 1),)] = zero_tall

        @pl.when(row == n_row - 1)
        def _():
            buf[at + (slice(2, 3),)] = zero_tall

        @pl.when(col == 0)
        def _():
            buf[at + (slice(None), slice(0, edge_g))] = zero_edge

        @pl.when(col == n_col - 1)
        def _():
            buf[at + (slice(None), slice(groups - edge_g, groups))] = zero_edge

    clear(packed, (2,))
    clear(packed_right, (1,))

    def flip(x):
        return jnp.concatenate([x[a : a + 1] for a in reversed(range(width))] + [x[width:]], axis=0)

    def build_tables():
        taps = kernel_ref[...]
        taps = jnp.concatenate([taps, jnp.zeros((width, LANES - width), jnp.float32)], axis=1)
        taps = jnp.concatenate([taps, jnp.zeros((LANES - width, LANES), jnp.float32)], axis=0)
        lines_ref[0] = pltpu.roll(flip(taps).T, LANES - width, axis=1)
        lines_ref[1] = pltpu.roll(taps.T, LANES - width, axis=1)

        for which in range(2):
            for q in range(2):
                for h in range(2):
                    for half in range(2):
                        lines = []
                        for g in range(4):
                            b = 16 * q + 8 * h + 4 * half + g
                            source = b - 1 if which == 0 else width - b
                            if b == 0:
                                lines.append(jnp.zeros((8, LANES), jnp.float32))
                            else:
                                lines.append(
                                    jnp.broadcast_to(lines_ref[which, source : source + 1, :], (8, LANES))
                                )
                        tiles = []
                        for k in range(2 * blk // 8):
                            pieces = [
                                pltpu.roll(
                                    lines[g], (blk * g + 8 * k) % LANES, axis=1, stride=1, stride_axis=0
                                )
                                for g in range(4)
                            ]
                            tiles.append(quarters(*pieces))
                        high, low = split(jnp.concatenate(tiles, axis=0))
                        at_row = pl.ds(LANES * q + 2 * blk * h, 2 * blk)
                        at_lane = pl.ds(LANES * half, LANES)
                        table[which, 0, at_row, at_lane] = high
                        table[which, 1, at_row, at_lane] = low

    def pack(tile):
        tall = jnp.concatenate([tile, pltpu.roll(tile, cols - 8, axis=1)], axis=0)
        pieces = [tall[:, k : k + LANES].T for k in range(0, cols, LANES)]
        form = jnp.concatenate(pieces, axis=0)
        return form.reshape(own_g, 2, 8, LANES)[:, 0]

    def expand(pk):
        after = jnp.concatenate([pk[1:], pk[:1]], axis=0)
        odd = jnp.where(low_half(pk.shape), after, pk).reshape(-1, LANES)
        odd = pltpu.roll(odd, LANES // 2, axis=1).reshape(pk.shape)
        return jnp.stack([pk, odd], axis=1).reshape(pk.shape[0] * 16, LANES)

    def strip(buf, sems, phase, index):
        dr, dc = DIRECTIONS[index]
        dst_strip = 1 - dr
        c_src, c_dst, c_len = (
            (edge_g, groups - edge_g, edge_g) if dc < 0
            else (groups - 2 * edge_g, 0, edge_g) if dc > 0
            else (edge_g, edge_g, own_g)
        )
        return pltpu.make_async_remote_copy(
            src_ref=buf.at[phase, 1, pl.ds(c_src, c_len)],
            dst_ref=buf.at[phase, 1 - (-dr), pl.ds(c_dst, c_len)] if False else buf.at[phase, dst_strip, pl.ds(c_dst, c_len)],
            send_sem=send_sem.at[sems, index],
            recv_sem=recv_sem.at[sems, index],
            device_id=(row + dr, col + dc),
            device_id_type=MESH,
        )

    def each(buf, sems, phase, act, sign):
        for index, (dr, dc) in enumerate(DIRECTIONS):
            pl.when(inside(sign * dr, sign * dc))(
                lambda index=index: act(strip(buf, sems, phase, index))
            )

    def send(buf, sems, phase):
        each(buf, sems, phase, lambda c: c.start(), 1)

    def receive(buf, sems, phase):
        each(buf, sems, phase, lambda c: c.wait_recv(), -1)

    def finish(buf, sems, phase):
        each(buf, sems, phase, lambda c: c.wait_send(), 1)

    first_row, last_row = row == 0, row == n_row - 1
    left_on = jnp.where(col == 0, 0.0, 1.0)
    right_on = jnp.where(col == n_col - 1, 0.0, 1.0)

    def row_mask(start):
        at = start + lax.rem(lane1, blk)
        off = jnp.logical_or(
            jnp.logical_and(at < 0, first_row), jnp.logical_and(at >= rows, last_row)
        )
        return jnp.where(off, 0.0, 1.0)

    def put_block(k, start, value, margin):
        if start < 0 or start + blk > rows:
            value = value * row_mask(start)
        n = value.shape[0]
        if margin:
            block_ref[k, 0:margin, :] = value[0:margin] * left_on
            block_ref[k, margin : n - margin, :] = value[margin : n - margin]
            block_ref[k, n - margin : n, :] = value[n - margin : n] * right_on
        else:
            block_ref[k, 0:n, :] = value

    def load_windows(n, n_in):
        for k in range(n):
            low_cols = [block_ref[k + j, 0:n_in, :] for j in range(2)]
            high_cols = [block_ref[k + j, 8 : n_in + 8, :] for j in range(2)]
            put_window(k, n_in, quarters(low_cols[0], low_cols[1], high_cols[0], high_cols[1]))

    def put_window(k, n_in, value):
        high, low = split(value)
        high_ref[k * n_in : (k + 1) * n_in, :] = high
        low_ref[k * n_in : (k + 1) * n_in, :] = low

    def convolve(which, n, n_in):
        m = n * n_in
        lhs = jnp.concatenate(
            [high_ref[0:m, :], high_ref[16 : m + 16, :], low_ref[0:m, :], low_ref[16 : m + 16, :],
             high_ref[0:m, :], high_ref[16 : m + 16, :]],
            axis=1,
        )
        rhs = jnp.concatenate([table[which, 0], table[which, 0], table[which, 1]], axis=0)
        out = jnp.dot(lhs, rhs, preferred_element_type=jnp.float32)
        wide0[0:m, :] = out[:, 0:LANES]
        wide1[0:m, :] = out[:, LANES:]

    def assemble(k, n_in):
        n_out = n_in - 2 * 16
        base = k * n_in
        partial_ref[0 : n_out + 8, :] = (
            wide0[base : base + n_out + 8, :] + wide1[base + 4 : base + n_out + 12, :]
        )
        total_ = quarters(*(partial_ref[j : j + n_out, :] for j in range(4)))
        total_ = total_ + pltpu.roll(total_, 2 * blk, axis=1)
        return total_ + pltpu.roll(total_, blk, axis=1)

    def window_sources(phase):
        up, mid, down = (expand(packed[phase, s]) for s in range(3))
        odd = lax.rem(lax.broadcasted_iota(jnp.int32, mid.shape, 1) // blk, 2) == 1
        upper = jnp.where(odd, pltpu.roll(mid, blk, axis=1), pltpu.roll(up, LANES - blk, axis=1))
        lower = jnp.where(odd, pltpu.roll(down, blk, axis=1), pltpu.roll(mid, LANES - blk, axis=1))
        natural = jnp.where(low_half(mid.shape), upper, pltpu.roll(lower, LANES // 2, axis=1))
        return (up, upper, mid, lower, down), natural

    def smooth(index, n_out):
        start = (total - n_out) // 2
        if index == 1:
            start = 16
        center = state_ref[index, start : start + n_out, :]
        left = state_ref[index, start - 1 : start - 1 + n_out, :]
        right = state_ref[index, start + 1 : start + 1 + n_out, :]
        upper = pltpu.roll(center, 1, axis=1)
        lower = pltpu.roll(center, LANES - 1, axis=1)
        return PENALTY * (4.0 * center - upper - lower - left - right)

    def merge(n):
        return quarters(*(block_ref[k, 0:n, :] for k in range(4)))

    def row_sum(x):
        return jnp.sum(x, axis=0, keepdims=True)

    own_lanes = jnp.logical_and(lane1 >= blk, lane1 < 3 * blk)

    def own(x):
        return jnp.where(own_lanes, x, 0.0)

    def first_half(phase):
        windows, natural = window_sources(phase)
        state_ref[0] = natural
        for k, w in enumerate(windows):
            put_window(k, total, w)
        convolve(0, 5, total)
        for k in range(5):
            put_block(k, -blk - 16 + blk * k, assemble(k, total), 48)
        load_windows(4, total - 32)
        convolve(1, 4, total - 32)
        for k in range(4):
            put_block(k, -blk + blk * k, assemble(k, total - 32), 32)

    def second_half_a():
        n_in = total - 64
        load_windows(3, n_in)
        convolve(0, 3, n_in)
        for k in range(3):
            put_block(k, -16 + blk * k, assemble(k, n_in), 16)

    def second_half_b():
        n_in = total - 96
        load_windows(2, n_in)
        convolve(1, 2, n_in)
        for k in range(2):
            block_ref[k, 0 : n_in - 32, :] = assemble(k, n_in)

    def masked_natural(value):
        at = lane1 - blk
        off = jnp.logical_or(
            jnp.logical_and(at < 0, first_row), jnp.logical_and(at >= rows, last_row)
        )
        value = value * jnp.where(off, 0.0, 1.0)
        n = value.shape[0]
        return jnp.concatenate(
            [value[0:32] * left_on, value[32 : n - 32], value[n - 32 :] * right_on], axis=0
        )

    def spill_natural(value):
        n = value.shape[0]
        turned = [value] + [pltpu.roll(value, LANES - blk * j, axis=1) for j in range(1, 4)]
        del n
        return turned

    def windows_from_natural(value):
        n = value.shape[0]
        after = jnp.concatenate([value[8:], value[:8]], axis=0)
        mask = low_half(value.shape)
        put_window(0, n, jnp.where(mask, value, pltpu.roll(after, LANES // 2, axis=1)))
        put_window(
            1, n,
            jnp.where(mask, pltpu.roll(value, LANES - blk, axis=1), pltpu.roll(after, blk, axis=1)),
        )
        put_window(2, n, jnp.where(mask, pltpu.roll(value, LANES // 2, axis=1), after))

    def finish_pair(index):
        parts = block_ref[0, 0:cols, :], block_ref[1, 0:cols, :]
        both = quarters(parts[0], parts[0], parts[1], parts[1])
        out = own(both + smooth_own())
        basis_ref[index] = out
        return out

    def smooth_own():
        start = 32
        center = state_ref[1, start : start + cols, :]
        left = state_ref[1, start - 1 : start - 1 + cols, :]
        right = state_ref[1, start + 1 : start + 1 + cols, :]
        upper = pltpu.roll(center, 1, axis=1)
        lower = pltpu.roll(center, LANES - 1, axis=1)
        return PENALTY * (4.0 * center - upper - lower - left - right)

    def smooth_wide():
        n_out = total - 64
        start = 32
        center = state_ref[0, start : start + n_out, :]
        left = state_ref[0, start - 1 : start - 1 + n_out, :]
        right = state_ref[0, start + 1 : start + 1 + n_out, :]
        upper = pltpu.roll(center, 1, axis=1)
        lower = pltpu.roll(center, LANES - 1, axis=1)
        return PENALTY * (4.0 * center - upper - lower - left - right)

    loads[0].wait()
    build_tables()
    loads[1].wait()
    packed[0, 1, edge_g : edge_g + own_g] = pack(guess_ref[...])
    loads[2].wait()
    packed_right[0, 1, edge_g : edge_g + own_g] = pack(right_ref[...])
    pl.semaphore_wait(barrier, count - 1)
    send(packed, 0, 0)
    send(packed_right, 1, 0)

    n_mid = total - 64
    receive(packed, 0, 0)
    first_half(0)
    receive(packed_right, 1, 0)
    up_r, mid_r, down_r = (expand(packed_right[0, s]) for s in range(3))
    sl = slice(32, 32 + n_mid)
    nat_r = jnp.where(
        low_half((n_mid, LANES)),
        jnp.where(
            lax.broadcasted_iota(jnp.int32, (n_mid, LANES), 1) < blk,
            pltpu.roll(up_r[sl], LANES - blk, axis=1),
            pltpu.roll(mid_r[sl], blk, axis=1),
        ),
        jnp.where(
            lax.broadcasted_iota(jnp.int32, (n_mid, LANES), 1) < 3 * blk,
            pltpu.roll(mid_r[sl], blk, axis=1),
            pltpu.roll(down_r[sl], 3 * blk, axis=1),
        ),
    )
    start_residual = masked_natural(nat_r - (merge(n_mid) + smooth_wide()))
    state_ref[1, 0:n_mid, :] = start_residual
    basis_ref[3] = own(state_ref[0, edge : edge + cols, :])
    r0 = own(start_residual[32 : 32 + cols])
    basis_ref[0] = r0
    windows_from_natural(start_residual)
    convolve(0, 3, n_mid)
    for k in range(3):
        put_block(k, -16 + blk * k, assemble(k, n_mid), 16)
    second_half_b()
    w1 = finish_pair(1)
    turned = pltpu.roll(w1, LANES - blk, axis=1).reshape(own_g, 2, 8, LANES)
    turned_up = pltpu.roll(w1, blk, axis=1).reshape(own_g, 2, 8, LANES)
    pk = jnp.where(low_half((own_g, 8, LANES)), turned[:, 0], turned_up[:, 1])
    packed[1, 1, edge_g : edge_g + own_g] = pk
    send(packed, 2, 1)
    finish(packed, 0, 0)
    finish(packed_right, 1, 0)
    m0, m1, m2 = row_sum(r0 * r0), row_sum(r0 * w1), row_sum(w1 * w1)

    receive(packed, 2, 1)
    first_half(1)
    second = masked_natural(merge(n_mid) + smooth_wide())
    state_ref[1, 0:n_mid, :] = second
    w2 = own(second[32 : 32 + cols])
    basis_ref[2] = w2
    m3, m4 = row_sum(basis_ref[1] * w2), row_sum(w2 * w2)
    windows_from_natural(second)
    convolve(0, 3, n_mid)
    for k in range(3):
        put_block(k, -16 + blk * k, assemble(k, n_mid), 16)
    k_rows = [block_ref[k, 16 : 16 + cols, :] for k in range(3)]
    joined = quarters(k_rows[0], k_rows[1], k_rows[2], k_rows[2])
    inside_k = jnp.logical_and(lane1 >= 16, lane1 < 16 + rows)
    joined = jnp.where(inside_k, joined, 0.0)
    smooth2 = smooth_own()
    m5 = row_sum(joined * joined) + row_sum(w2 * smooth2)

    def fold(x):
        for k in (64, 32, 16):
            x = x + pltpu.roll(x, k, axis=1)
        return x

    line = jnp.zeros((1, LANES), jnp.float32)
    for k, m in enumerate((m0, m1, m2, m3, m4, m5)):
        at_k = jnp.logical_and(lane1 >= 16 * k, lane1 < 16 * (k + 1))
        line = jnp.where(at_k, fold(m), line)
    red[me] = line

    def red_copy(place):
        return pltpu.make_async_remote_copy(
            src_ref=red.at[me], dst_ref=red.at[me], send_sem=red_send.at[0], recv_sem=red_recv.at[0],
            device_id=place, device_id_type=MESH,
        )

    all_red = pltpu.make_async_remote_copy(
        src_ref=red.at[pl.ds(0, count - 1)], dst_ref=red.at[pl.ds(0, count - 1)],
        send_sem=red_send.at[0], recv_sem=red_recv.at[0],
        device_id=(row, col), device_id_type=MESH,
    )
    others(lambda place: red_copy(place).start())
    finish(packed, 2, 1)
    second_half_b()
    w3 = finish_pair(4)

    all_red.wait_recv()
    sums = jnp.sum(red[...], axis=0)
    m = [
        jnp.sum(
            jnp.where(jnp.logical_and(lane1 >= 16 * k, lane1 < 16 * (k + 1)), sums, 0.0),
            axis=1, keepdims=True,
        )
        for k in range(MOMENTS)
    ]

    def times(p, q):
        return sum(
            p[i] * q[j] * m[i + j] for i in range(len(p)) for j in range(len(q))
        )

    rho, pi = [jnp.ones((1, 1), jnp.float32)], [jnp.ones((1, 1), jnp.float32)]
    step_sum = []
    norm = m[0]
    for it in range(3):
        shifted = [jnp.zeros((1, 1), jnp.float32)] + pi
        alpha = norm / times(pi, shifted)
        step_sum = [
            (step_sum[i] if i < len(step_sum) else 0.0) + alpha * pi[i] for i in range(len(pi))
        ]
        rho = [
            (rho[i] if i < len(rho) else 0.0) - alpha * shifted[i] for i in range(len(shifted))
        ]
        if it < 2:
            norm_next = times(rho, rho)
            beta = norm_next / norm
            pi = [rho[i] + (beta * pi[i] if i < len(pi) else 0.0) for i in range(len(rho))]
            norm = norm_next

    r0, w1, w2 = basis_ref[0], basis_ref[1], basis_ref[2]
    template = basis_ref[3] + step_sum[0] * r0 + step_sum[1] * w1 + step_sum[2] * w2
    residual = rho[0] * r0 + rho[1] * w1 + rho[2] * w2 + rho[3] * w3
    for ref, value in ((template_ref, template), (residual_ref, residual)):
        for k in range(0, cols, LANES):
            ref[:, k : k + LANES] = value[k : k + LANES].T[blk : blk + rows]
    all_red.wait_send()


def on_device(n_row, n_col, right_side, initial_guess, kernel):
    rows, cols = right_side.shape
    total = cols + 2 * rows
    count = n_row * n_col
    shape = jax.ShapeDtypeStruct((rows, cols), jnp.float32)
    f32, bf16 = jnp.float32, jnp.bfloat16
    copies = len(DIRECTIONS)
    return pl.pallas_call(
        functools.partial(body, n_row, n_col),
        out_shape=(shape, shape),
        in_specs=[pl.BlockSpec(memory_space=pl.ANY)] * 3,
        out_specs=[pl.BlockSpec(memory_space=pltpu.VMEM)] * 2,
        scratch_shapes=[
            pltpu.VMEM((rows, cols), f32),
            pltpu.VMEM((rows, cols), f32),
            pltpu.VMEM(kernel.shape, f32),
            pltpu.VMEM((2, 3, total // 16, 8, LANES), f32),
            pltpu.VMEM((1, 3, total // 16, 8, LANES), f32),
            pltpu.VMEM((2, LANES, LANES), f32),
            pltpu.VMEM((2, 2, 2 * LANES, 2 * LANES), bf16),
            pltpu.VMEM((5 * total + 16, LANES), bf16),
            pltpu.VMEM((5 * total + 16, LANES), bf16),
            pltpu.VMEM((5 * total + 16, LANES), f32),
            pltpu.VMEM((5 * total + 16, LANES), f32),
            pltpu.VMEM((total, LANES), f32),
            pltpu.VMEM((5, total + 8, LANES), f32),
            pltpu.VMEM((2, total, LANES), f32),
            pltpu.VMEM((5, cols, LANES), f32),
            pltpu.VMEM((count, 1, LANES), f32),
            pltpu.SemaphoreType.DMA((3,)),
            pltpu.SemaphoreType.DMA((3, copies)),
            pltpu.SemaphoreType.DMA((3, copies)),
            pltpu.SemaphoreType.DMA((1,)),
            pltpu.SemaphoreType.DMA((1,)),
        ],
        compiler_params=pltpu.CompilerParams(collective_id=0, has_side_effects=True),
    )(right_side, initial_guess, kernel)


def solution(mesh):
    placed = (P("row", "col"), P("row", "col"), P())
    return jax.shard_map(
        functools.partial(on_device, mesh.shape["row"], mesh.shape["col"]),
        mesh=mesh,
        in_specs=placed,
        out_specs=(P("row", "col"), P("row", "col")),
        check_vma=False,
    )
```

time: 51.5 us -> 35.5 us (0.69)
  Pallas kernels: 48.5 us -> 32.4 us
    pallas_call x1, Pallas kernels: 48.5 us -> 32.4 us  [on_device(): pl.pallas_call(functools.partial(body, n_row, n_col), out_shape=(shape, s...]
where the time goes in v1:
time: 35.5 us; the launch traced here: 35.2 us
  Pallas kernels  32.4 us (91%)
  local copies, waits for them, and re-layouts  2.14 us (6%)
  between operations  0.65 us (2%)
    pallas_call x1, Pallas kernels, on_device(): pl.pallas_call(functools.partial(body, n_row, n_col), out_shape=(shape, s...  32.4 us
    unnamed x4, local copies, waits for them, and re-layouts  2.14 us

profile of v1, /device:TPU:0, one launch (start us, length us, event | category | flops | bytes accessed | tf_op | source)
XLA Modules:
  0.0 35.2 jit_solution(15474449200789534118)
XLA Ops:
  0.6 32.4 %shard_map.50 = (f32[64,256]{1,0:T(8,128)}, f32[64,256]{1,0:T(8,128)}) custom-call(f32[64,256]{1,0:T(8,128)} %right_hbm.1, f32[64,256]{1,0:T(8,128)} %guess_hbm.1, f32[31,31]{1,0:T(8,128)} %kernel_hbm.1), custom_call_target="tpu_custom_call" | custom-call | tf_op jit(solution)/shard_map/pallas_call | solution.py:499
  33.1 0.0 copy-start
  33.1 1.5 %copy.7 = f32[64,256]{1,0:T(8,128)} copy(f32[64,256]{1,0:T(8,128)} %get-tuple-element.4) | data formatting | bytes 131072
  34.6 0.0 copy-done
  34.6 0.6 %copy.8 = f32[64,256]{1,0:T(8,128)} copy(f32[64,256]{1,0:T(8,128)S(1)} %copy-done) | data formatting | bytes 131072
Async XLA Ops:
  33.1 1.5 %copy-start = (f32[64,256]{1,0:T(8,128)S(1)}, f32[64,256]{1,0:T(8,128)}, u32[]{:S(2)}) copy-start(f32[64,256]{1,0:T(8,128)} %get-tuple-element.5) | copy-start | bytes 196612

commit v2 on v1

--- a/solution.py
+++ b/solution.py
@@ -20,8 +20,17 @@
     return high, low
 
 
-def body(
-    n_row, n_col,
+def body(n_row, n_col, *refs):
+    pieces = [pltpu.ACC(unit)((16, 256), jnp.float32) for unit in range(2) for _ in range(64)]
+
+    def inner(*accs):
+        run(n_row, n_col, (accs[:64], accs[64:]), *refs)
+
+    pl.run_scoped(inner, *pieces)
+
+
+def run(
+    n_row, n_col, accs,
     right_hbm, guess_hbm, kernel_hbm, template_ref, residual_ref,
     right_ref, guess_ref, kernel_ref, packed, packed_right, lines_ref, table, high_ref, low_ref,
     wide0, wide1, partial_ref, block_ref, state_ref, basis_ref, red,
@@ -220,17 +229,34 @@
         high_ref[k * n_in : (k + 1) * n_in, :] = high
         low_ref[k * n_in : (k + 1) * n_in, :] = low
 
+    next_piece = [0, 0]
+
+    def take(unit):
+        acc = accs[unit][next_piece[unit] % len(accs[unit])]
+        next_piece[unit] += 1
+        return acc
+
     def convolve(which, n, n_in):
-        m = n * n_in
-        lhs = jnp.concatenate(
-            [high_ref[0:m, :], high_ref[16 : m + 16, :], low_ref[0:m, :], low_ref[16 : m + 16, :],
-             high_ref[0:m, :], high_ref[16 : m + 16, :]],
-            axis=1,
-        )
-        rhs = jnp.concatenate([table[which, 0], table[which, 0], table[which, 1]], axis=0)
-        out = jnp.dot(lhs, rhs, preferred_element_type=jnp.float32)
-        wide0[0:m, :] = out[:, 0:LANES]
-        wide1[0:m, :] = out[:, LANES:]
+        units = (n_in - 16) // 16
+        for k in range(n):
+            cut = (units + 1 - k % 2) // 2
+            share = (range(0, cut), range(cut, units))
+            held = [[take(unit) for _ in share[unit]] for unit in range(2)]
+            for part in range(2):
+                for unit in range(2):
+                    pltpu.matmul_push_rhs(table[which, part], staging_register=part, mxu_index=unit)
+            for source, load in ((high_ref, 0), (low_ref, None), (high_ref, 1)):
+                for unit in range(2):
+                    for i, (u, acc) in enumerate(zip(share[unit], held[unit])):
+                        at = k * n_in + 16 * u
+                        lhs = jnp.concatenate([source[at : at + 16, :], source[at + 16 : at + 32, :]], axis=1)
+                        pltpu.matmul_acc_lhs(acc, lhs, load_staged_rhs=load if i == 0 else None)
+            for unit in range(2):
+                for u, acc in zip(share[unit], held[unit]):
+                    out = pltpu.matmul_pop(acc)
+                    at = k * n_in + 16 * u
+                    wide0[at : at + 16, :] = out[:, 0:LANES]
+                    wide1[at : at + 16, :] = out[:, LANES:]
 
     def assemble(k, n_in):
         n_out = n_in - 2 * 16

time: 35.5 us -> 31.3 us (0.88)
  Pallas kernels: 32.4 us -> 28.2 us
    pallas_call x1, Pallas kernels: 32.4 us -> 28.2 us  [on_device(): pl.pallas_call(functools.partial(body, n_row, n_col), out_shape=(shape, s...]
where the time goes in v2:
time: 31.3 us; the launch traced here: 31 us
  Pallas kernels  28.2 us (90%)
  local copies, waits for them, and re-layouts  2.14 us (7%)
  between operations  0.65 us (2%)
    pallas_call x1, Pallas kernels, on_device(): pl.pallas_call(functools.partial(body, n_row, n_col), out_shape=(shape, s...  28.2 us
    unnamed x4, local copies, waits for them, and re-layouts  2.14 us

profile of v2, /device:TPU:0, one launch (start us, length us, event | category | flops | bytes accessed | tf_op | source)
XLA Modules:
  0.0 31.0 jit_solution(3601761982694364570)
XLA Ops:
  0.6 28.2 %shard_map.50 = (f32[64,256]{1,0:T(8,128)}, f32[64,256]{1,0:T(8,128)}) custom-call(f32[64,256]{1,0:T(8,128)} %refs_0_.1, f32[64,256]{1,0:T(8,128)} %refs_1_.1, f32[31,31]{1,0:T(8,128)} %refs_2_.1), custom_call_target="tpu_custom_call" | custom-call | tf_op jit(solution)/shard_map/pallas_call | solution.py:525
  28.9 0.0 copy-start
  28.9 1.5 %copy.7 = f32[64,256]{1,0:T(8,128)} copy(f32[64,256]{1,0:T(8,128)} %get-tuple-element.4) | data formatting | bytes 131072
  30.4 0.0 copy-done
  30.4 0.6 %copy.8 = f32[64,256]{1,0:T(8,128)} copy(f32[64,256]{1,0:T(8,128)S(1)} %copy-done) | data formatting | bytes 131072
Async XLA Ops:
  28.9 1.5 %copy-start = (f32[64,256]{1,0:T(8,128)S(1)}, f32[64,256]{1,0:T(8,128)}, u32[]{:S(2)}) copy-start(f32[64,256]{1,0:T(8,128)} %get-tuple-element.5) | copy-start | bytes 196612

commit v3 on v0

v3 whole, which is shorter than its diff:
```python
import functools

import jax
import jax.numpy as jnp
from jax import lax
from jax.experimental import pallas as pl
from jax.experimental.pallas import tpu as pltpu
from jax.sharding import PartitionSpec as P

PENALTY = 0.05
LANES = 128
PIECE = 16
PIECES = 64
STEPS = (8, 15, 20)
SUMS = 9
MESH = pl.DeviceIdType.MESH
DIRECTIONS = ((-1, 0), (1, 0), (-1, -1), (-1, 1), (1, -1), (1, 1), (0, -1), (0, 1))


NEAR = tuple((a, b) for a in (-1, 0, 1) for b in (-1, 0, 1) if (a, b) != (0, 0))
GREET = NEAR + ((0, -4), (0, 4))


def square(r, c):
    return tuple((a, b) for a in (-r, 0, r) for b in (-c, 0, c) if (a, b) != (0, 0))


def greetings(n_row, n_col):
    places = [(r, c) for r in range(n_row) for c in range(n_col)]

    def reach(place, offsets):
        near = ((place[0] + a, place[1] + b) for a, b in offsets)
        return [p for p in near if 0 <= p[0] < n_row and 0 <= p[1] < n_col]

    def hear(known, offsets):
        if any(p not in known[d] for d in places for p in reach(d, offsets)):
            return None
        return {d: known[d].union(*(known[p] for p in reach(d, offsets))) for d in places}

    known = {d: {d, *reach(d, GREET)} for d in places}
    known = hear(known, NEAR)
    rounds = []
    while min(map(len, known.values())) < len(places):
        best = None
        for r in range(1, max(2, n_row)):
            for c in range(1, max(2, n_col)):
                after = hear(known, square(r, c))
                if after is not None:
                    score = (min(map(len, after.values())), -r - c)
                    if best is None or score > best[0]:
                        best = (score, square(r, c), after)
        rounds.append(best[1])
        known = best[2]
    return rounds


def split(x):
    high = x.astype(jnp.bfloat16)
    low = (x - high.astype(jnp.float32)).astype(jnp.bfloat16)
    return high, low


def body(n_row, n_col, *refs):
    pieces = [
        pltpu.ACC(unit)((PIECE, 2 * LANES), jnp.float32) for unit in range(2) for _ in range(PIECES)
    ]

    def inner(*accs):
        run(n_row, n_col, (accs[:PIECES], accs[PIECES:]), *refs)

    pl.run_scoped(inner, *pieces)


def run(
    n_row, n_col, accs,
    right_hbm, guess_hbm, kernel_hbm, template_ref, residual_ref,
    right_ref, guess_ref, kernel_ref, first_pack, right_pack, second_pack,
    lines_ref, table, high_ref, low_ref, wide, partial_ref,
    state_ref, right_nat, own_ref, red, load_sem, send_sem, recv_sem, red_send, red_recv, known_sem,
):
    rows, cols = right_ref.shape
    row, col = lax.axis_index("row"), lax.axis_index("col")
    me, count = row * n_col + col, n_row * n_col
    width = kernel_ref.shape[0]
    blk = rows // 2
    own_g = cols // PIECE

    barrier = pltpu.get_barrier_semaphore()

    def within(dr, dc):
        return jnp.logical_and(
            jnp.logical_and(row + dr >= 0, row + dr < n_row),
            jnp.logical_and(col + dc >= 0, col + dc < n_col),
        )

    def greet(sem, offsets):
        for dr, dc in offsets:
            pl.when(within(dr, dc))(
                lambda dr=dr, dc=dc: pl.semaphore_signal(
                    sem, inc=1, device_id=(row + dr, col + dc), device_id_type=MESH
                )
            )

    def heard(offsets):
        return functools.reduce(jnp.add, [jnp.where(within(dr, dc), 1, 0) for dr, dc in offsets])

    greet(barrier, GREET)
    loads = [
        pltpu.make_async_copy(src, dst, load_sem.at[k])
        for k, (src, dst) in enumerate(
            ((guess_hbm, guess_ref), (right_hbm, right_ref), (kernel_hbm, kernel_ref))
        )
    ]
    for load in loads:
        load.start()

    lane1 = lax.broadcasted_iota(jnp.int32, (1, LANES), 1)

    def lanes_of(shape):
        return lax.broadcasted_iota(jnp.int32, shape, len(shape) - 1)

    def low_half(x):
        return lanes_of(x.shape) < LANES // 2

    def quarters(a, b, c, d):
        q = lanes_of(a.shape)
        return jnp.where(
            q < 2 * blk, jnp.where(q < blk, a, b), jnp.where(q < 3 * blk, c, d)
        )

    def turn(x, by):
        return pltpu.roll(x, by % LANES, axis=1)

    def inside(dr, dc):
        checks = []
        if dr:
            checks.append(row + dr >= 0 if dr < 0 else row + dr < n_row)
        if dc:
            checks.append(col + dc >= 0 if dc < 0 else col + dc < n_col)
        return functools.reduce(jnp.logical_and, checks)

    def clear(buf):
        groups = buf.shape[1]
        edge = (groups - own_g) // 2

        @pl.when(row == 0)
        def _():
            buf[0] = jnp.zeros(buf.shape[1:], jnp.float32)

        @pl.when(row == n_row - 1)
        def _():
            buf[2] = jnp.zeros(buf.shape[1:], jnp.float32)

        @pl.when(col == 0)
        def _():
            buf[:, 0:edge] = jnp.zeros((3, edge, 8, LANES), jnp.float32)

        @pl.when(col == n_col - 1)
        def _():
            buf[:, groups - edge : groups] = jnp.zeros((3, edge, 8, LANES), jnp.float32)

    def each(buf, turn_no, act, sign):
        groups = buf.shape[1]
        edge = (groups - own_g) // 2

        def one(index):
            dr, dc = DIRECTIONS[index]
            c_src, c_dst, c_len = (
                (edge, groups - edge, edge) if dc < 0
                else (own_g, 0, edge) if dc > 0
                else (edge, edge, own_g)
            )
            act(pltpu.make_async_remote_copy(
                src_ref=buf.at[1, pl.ds(c_src, c_len)],
                dst_ref=buf.at[1 - dr, pl.ds(c_dst, c_len)],
                send_sem=send_sem.at[turn_no, index],
                recv_sem=recv_sem.at[turn_no, index],
                device_id=(row + dr, col + dc),
                device_id_type=MESH,
            ))

        for index, (dr, dc) in enumerate(DIRECTIONS):
            pl.when(inside(sign * dr, sign * dc))(functools.partial(one, index))

    def send(buf, turn_no):
        each(buf, turn_no, lambda c: c.start(), 1)

    def receive(buf, turn_no):
        each(buf, turn_no, lambda c: c.wait_recv(), -1)

    def finish(buf, turn_no):
        each(buf, turn_no, lambda c: c.wait_send(), 1)

    def flip(x):
        return jnp.concatenate([x[a : a + 1] for a in reversed(range(width))] + [x[width:]], axis=0)

    def build_tables():
        taps = kernel_ref[...]
        taps = jnp.concatenate([taps, jnp.zeros((width, LANES - width), jnp.float32)], axis=1)
        taps = jnp.concatenate([taps, jnp.zeros((LANES - width, LANES), jnp.float32)], axis=0)
        lines_ref[0] = turn(flip(taps).T, -width)
        lines_ref[1] = turn(taps.T, -width)

        for which in range(2):
            for q in range(2):
                for h in range(2):
                    for half in range(2):
                        lines = []
                        for g in range(4):
                            b = 16 * q + 8 * h + 4 * half + g
                            source = b - 1 if which == 0 else width - b
                            if b == 0:
                                lines.append(jnp.zeros((8, LANES), jnp.float32))
                            else:
                                lines.append(
                                    jnp.broadcast_to(lines_ref[which, source : source + 1, :], (8, LANES))
                                )
                        tiles = []
                        for k in range(2 * blk // 8):
                            tiles.append(quarters(*(
                                pltpu.roll(
                                    lines[g], (blk * g + 8 * k) % LANES, axis=1, stride=1, stride_axis=0
                                )
                                for g in range(4)
                            )))
                        high, low = split(jnp.concatenate(tiles, axis=0))
                        at_row = pl.ds(LANES * q + 2 * blk * h, 2 * blk)
                        at_lane = pl.ds(LANES * half, LANES)
                        table[which, 0, at_row, at_lane] = high
                        table[which, 1, at_row, at_lane] = low

    def pack(tile):
        tall = jnp.concatenate([tile, pltpu.roll(tile, cols - 8, axis=1)], axis=0)
        pieces = [tall[:, k : k + LANES].T for k in range(0, cols, LANES)]
        form = jnp.concatenate(pieces, axis=0)
        return form.reshape(own_g, 2, 8, LANES)[:, 0]

    def expand(buf, tile, first, size):
        last = min(first + size, buf.shape[1] - 1)
        pk = buf[tile, first : first + size]
        after = buf[tile, last : last + 1]
        if size > 1:
            after = jnp.concatenate([pk[1:], after], axis=0)
        odd = jnp.where(low_half(pk), after, pk).reshape(-1, LANES)
        odd = turn(odd, LANES // 2).reshape(pk.shape)
        return jnp.stack([pk, odd], axis=1).reshape(size * 16, LANES)

    first_row, last_row = row == 0, row == n_row - 1
    left_on = jnp.where(col == 0, 0.0, 1.0)
    right_on = jnp.where(col == n_col - 1, 0.0, 1.0)

    def row_mask(at):
        off = jnp.logical_or(
            jnp.logical_and(at < 0, first_row), jnp.logical_and(at >= rows, last_row)
        )
        return jnp.where(off, 0.0, 1.0)

    def masked(value, start, margin, mask):
        out = []
        for j in range(start, start + value.shape[0], PIECE):
            piece = value[j - start : j - start + PIECE]
            side = mask
            if j < margin:
                side = mask * left_on
            elif j >= margin + cols:
                side = mask * right_on
            out.append(piece * side)
        return jnp.concatenate(out, axis=0) if len(out) > 1 else out[0]

    counters = {"piece": [0, 0], "stage": 0}

    def take(unit):
        acc = accs[unit][counters["piece"][unit] % PIECES]
        counters["piece"][unit] += 1
        return acc

    def put_window(slot, k, at, value):
        high, low = split(value)
        high_ref[slot, k, at : at + value.shape[0], :] = high
        low_ref[slot, k, at : at + value.shape[0], :] = low

    class Stage:
        def __init__(self, which, n, n_in, lag, emit, feed=None, before=None):
            self.which, self.n, self.n_in, self.emit, self.feed = which, n, n_in, emit, feed
            self.before = before
            self.slot = counters["stage"] % 2
            counters["stage"] += 1
            self.units, self.n_out = (n_in - 16) // PIECE, n_in - 32
            self.ends = [e for e in (step - lag for step in STEPS) if 0 < e < self.units] + [self.units]
            self.starts = [0] + self.ends[:-1]
            self.done_t = self.done_o = 0

        def cost(self, i):
            return self.n * ((self.ends[i] - self.starts[i] + 1) // 2) * 24

        def matmul(self, i):
            c0, c1, slot, n = self.starts[i], self.ends[i], self.slot, self.n
            if i == 0 and self.before is not None:
                self.before()
            if self.feed is not None:
                self.feed(slot, c1 * PIECE + PIECE)
            middle = (c0 + c1 + (i + 1) % 2) // 2
            share = (range(c0, middle), range(middle, c1))
            held = [[(k, u, take(unit)) for k in range(n) for u in share[unit]] for unit in range(2)]
            for part in range(2):
                for unit in range(2):
                    if held[unit]:
                        pltpu.matmul_push_rhs(
                            table[self.which, part], staging_register=part, mxu_index=unit
                        )
            for source, load in ((high_ref, 0), (low_ref, None), (high_ref, 1)):
                for unit in range(2):
                    for j, (k, u, acc) in enumerate(held[unit]):
                        at = PIECE * u
                        lhs = jnp.concatenate(
                            [source[slot, k, at : at + 16, :], source[slot, k, at + 16 : at + 32, :]], axis=1
                        )
                        pltpu.matmul_acc_lhs(acc, lhs, load_staged_rhs=load if j == 0 else None)
            self.held = held

        def pop(self):
            slot = self.slot
            for unit in range(2):
                for k, u, acc in self.held[unit]:
                    out = pltpu.matmul_pop(acc)
                    at = PIECE * u
                    wide[slot, 0, k, at : at + PIECE, :] = out[:, 0:LANES]
                    wide[slot, 1, k, at : at + PIECE, :] = out[:, LANES:]

        def vector(self, i):
            slot = self.slot
            rows_done = self.ends[i] * PIECE
            t0, t1 = self.done_t, rows_done - 8
            for k in range(self.n):
                partial_ref[slot, k, t0:t1, :] = wide[slot, 0, k, t0:t1, :] + wide[slot, 1, k, t0 + 4 : t1 + 4, :]
            self.done_t = t1
            o1 = min(rows_done - 16, self.n_out)
            o = self.done_o
            while o < o1:
                e = min(o - o % 32 + 32, o1)
                self.emit(1 - slot, o, e, functools.partial(taken, slot, o, e))
                o = e
            self.done_o = o1

    def pipeline(stages):
        lag = 540
        next_mm = [0] * len(stages)
        done = [[] for _ in stages]
        clock, pending = 0, []
        while any(n < len(st.ends) for n, st in zip(next_mm, stages)):
            options = []
            for s, st in enumerate(stages):
                i = next_mm[s]
                if i == len(st.ends):
                    continue
                ready = 0
                if s:
                    need = st.ends[i] + 3 if i + 1 < len(st.ends) else stages[s - 1].units
                    before = [t for e, t in zip(stages[s - 1].ends, done[s - 1]) if e >= need]
                    if not before:
                        continue
                    ready = before[0]
                options.append((max(ready, clock), s))
            start, s = min(options)
            st, i = stages[s], next_mm[s]
            for item in [p for p in pending if p[0] <= start]:
                item[1].vector(item[2])
                pending.remove(item)
            st.matmul(i)
            st.pop()
            next_mm[s] += 1
            clock = start + st.cost(i)
            done[s].append(clock + lag)
            pending.append((clock + 200, st, i))
        for item in pending:
            item[1].vector(item[2])

    def taken(slot, o, e, k, shift):
        return partial_ref[slot, k, o + shift : e + shift, :]

    def fold4(t, *source):
        out = 0.0
        for s in range(4):
            out = out + turn(quarters(*(t(source[(p + s) % 4], p) for p in range(4))), s * blk)
        return out

    class Windows:
        def __init__(self, n):
            self.n, self.kept, self.at = n, None, 0

        def make(self, slot, parts):
            size = parts[0].shape[0] - 16
            if self.n == 2:
                for k in range(2):
                    a, b = parts[k], parts[k + 1]
                    win = quarters(a[0:size], b[0:size], a[8 : size + 8], b[8 : size + 8])
                    put_window(slot, k, self.at, win)
                self.at += size
                return
            value, t32, t64, t96, extra = parts

            def lo(x):
                return x[0:size]

            def hi(x):
                return x[8 : size + 8]

            for k in range(self.n):
                if k == 0:
                    win = jnp.where(low_half(lo(value)), lo(value), hi(t64))
                elif k == 1:
                    win = jnp.where(low_half(lo(value)), lo(t96), hi(t32))
                elif k == 2:
                    win = jnp.where(low_half(lo(value)), lo(t64), hi(value))
                else:
                    win = quarters(lo(t32), lo(extra), hi(t96), hi(extra))
                put_window(slot, k, self.at, win)
            self.at += size

        def add(self, slot, value, extra=None):
            if self.n == 2:
                parts = value
            else:
                parts = [value, turn(value, blk), turn(value, 2 * blk), turn(value, 3 * blk), extra]
            if self.kept is not None:
                parts = [
                    None if new is None else jnp.concatenate([old, new], axis=0)
                    for old, new in zip(self.kept, parts)
                ]
            if parts[0].shape[0] > 16:
                self.make(slot, parts)
            self.kept = [None if p is None else p[p.shape[0] - 16 :] for p in parts]

        def end(self, slot):
            parts = [None if p is None else jnp.concatenate([p, p], axis=0) for p in self.kept]
            self.make(slot, parts)

    def smooth(index, start, end):
        center = state_ref[index, start:end, :]
        left = state_ref[index, start - 1 : end - 1, :]
        right = state_ref[index, start + 1 : end + 1, :]
        return PENALTY * (4.0 * center - turn(center, 1) - turn(center, -1) - left - right)

    def repack(buf, group, value):
        n = value.shape[0] // 16
        down, up = (turn(value, by).reshape(n, 2, 8, LANES) for by in (-blk, blk))
        buf[1, group : group + n] = jnp.where(low_half(down[:, 0]), down[:, 0], up[:, 1])

    class Feed:
        def __init__(self, buf):
            self.buf, self.at = buf, 0

        def __call__(self, slot, upto):
            upto = min(upto, self.buf.shape[1] * 16)
            while self.at < upto:
                self.two(slot, self.at // 16, min(2, (upto - self.at) // 16))

        def two(self, slot, first, size):
            up, mid, down = (expand(self.buf, s, first, size) for s in range(3))
            at = self.at
            odd = lax.rem(lanes_of(mid.shape), 2 * blk) >= blk
            upper = jnp.where(odd, turn(mid, blk), turn(up, -blk))
            lower = jnp.where(odd, turn(down, blk), turn(mid, -blk))
            for k, w in enumerate((up, upper, mid, lower, down)):
                put_window(slot, k, at, w)
            state_ref[0, at : at + size * 16, :] = jnp.where(low_half(mid), upper, turn(lower, 2 * blk))
            self.at += size * 16

    def row_sum(x):
        return jnp.sum(x, axis=0, keepdims=True)

    def red_copy(turn_no, place):
        return pltpu.make_async_remote_copy(
            src_ref=red.at[turn_no, me], dst_ref=red.at[turn_no, me],
            send_sem=red_send.at[turn_no], recv_sem=red_recv.at[turn_no],
            device_id=place, device_id_type=MESH,
        )

    def all_red(turn_no):
        return pltpu.make_async_remote_copy(
            src_ref=red.at[turn_no, pl.ds(0, count - 1)], dst_ref=red.at[turn_no, pl.ds(0, count - 1)],
            send_sem=red_send.at[turn_no], recv_sem=red_recv.at[turn_no],
            device_id=(row, col), device_id_type=MESH,
        )

    def flipped(x, n, bits):
        if n & (n - 1):
            return lax.rem(x + bits, n)
        for k in range(n.bit_length() - 1):
            if bits >> k & 1:
                x = x + (1 - 2 * lax.rem(x // (1 << k), 2)) * (1 << k)
        return x

    def spread(turn_no, line):
        red[turn_no, me] = line
        for r in reversed(range(n_row)):
            for c in reversed(range(n_col)):
                if r or c:
                    red_copy(turn_no, (flipped(row, n_row, r), flipped(col, n_col, c))).start()

    def gather(turn_no, groups):
        all_red(turn_no).wait_recv()
        line = jnp.sum(red[turn_no], axis=0)
        return [
            jnp.sum(
                jnp.where(jnp.logical_and(lane1 >= a, lane1 < b), line, 0.0), axis=1, keepdims=True
            )
            for a, b in groups
        ]

    right_groups = right_pack.shape[1]
    first_row_at, last_row_at = row == 0, row == n_row - 1

    def blank(where):
        right_pack[where] = jnp.zeros_like(right_pack[where])

    def right_form(half, s):
        x = right_ref[half * blk : half * blk + blk, :]
        tall = jnp.concatenate(
            [x if p == s else pltpu.roll(x, cols - 8 * ((p - s) % 4), axis=1) for p in range(4)], axis=0
        )
        pieces = [tall[:, k : k + LANES].T for k in range(0, cols, LANES)]
        return jnp.concatenate(pieces, axis=0).reshape(right_groups - 2, 4, 8, LANES)[:, 0]

    def each_right(act, sign):
        def one(index):
            dr, dc = DIRECTIONS[index]
            src, dst = {-1: (4, 3), 1: (5, 0), 0: (1, 1)}[dr]
            c_src, c_dst, c_len = (
                (1, right_groups - 1, 1) if dc < 0
                else (right_groups - 2, 0, 1) if dc > 0
                else (1, 1, right_groups - 2)
            )
            planes = 1 if dr else 2
            act(pltpu.make_async_remote_copy(
                src_ref=right_pack.at[pl.ds(src, planes), pl.ds(c_src, c_len)],
                dst_ref=right_pack.at[pl.ds(dst, planes), pl.ds(c_dst, c_len)],
                send_sem=send_sem.at[1, index],
                recv_sem=recv_sem.at[1, index],
                device_id=(row + dr, col + dc),
                device_id_type=MESH,
            ))

        for index, (dr, dc) in enumerate(DIRECTIONS):
            pl.when(inside(sign * dr, sign * dc))(functools.partial(one, index))

    def right_natural():
        each_right(lambda c: c.wait_recv(), -1)
        planes = [right_pack[k] for k in range(4)]
        for t in range(4):
            value = quarters(*(planes[(p - t) % 4].reshape(-1, LANES) for p in range(4)))
            right_nat[:, t] = turn(value, -blk * t).reshape(right_groups, 8, LANES)

    clear(first_pack)
    for at_edge, where in (
        (first_row_at, (slice(0, 1), slice(None))), (last_row_at, (slice(3, 4), slice(None))),
        (col == 0, (slice(0, 4), slice(0, 1))),
        (col == n_col - 1, (slice(0, 4), slice(right_groups - 1, right_groups))),
    ):
        pl.when(at_edge)(functools.partial(blank, where))
    clear(second_pack)
    edge1 = (first_pack.shape[1] - own_g) // 2
    edge2 = (second_pack.shape[1] - own_g) // 2
    loads[0].wait()
    first_pack[1, edge1 : edge1 + own_g] = pack(guess_ref[...])
    pl.semaphore_wait(barrier, heard(GREET))
    send(first_pack, 0)
    loads[1].wait()
    for plane, half, s in ((4, 0, 3), (5, 1, 0), (1, 0, 1), (2, 1, 2)):
        right_pack[plane, 1 : right_groups - 1] = right_form(half, s)
    each_right(lambda c: c.start(), 1)
    loads[2].wait()
    build_tables()

    mask48, mask32 = (row_mask(lane1 - k) for k in (48, 32))
    mask_low = row_mask(rows + 16 + 0 * lane1)
    masks16 = [row_mask(blk * k - 16 + lax.rem(lane1, blk)) for k in range(3)]
    own32 = jnp.logical_and(lane1 >= 32, lane1 < 32 + rows)
    own16 = jnp.logical_and(lane1 >= 16, lane1 < 16 + rows)
    dots = [0.0] * SUMS
    first_sums = [0.0, 0.0]
    n_in = first_pack.shape[1] * 16

    def own_part(o, e, margin):
        a, b = max(o, margin), min(e, margin + cols)
        return slice(a - margin, b - margin), slice(a - o, b - o), a < b

    step = {}

    def late_wait():
        step["m0"], step["m1"] = gather(0, ((0, 64), (64, 128)))
        step["alpha0"] = step["m0"] / step["m1"]

    def three_stages(buf, second):
        wins_b, wins_c, wins_d = Windows(4), Windows(3), Windows(2)

        def emit_a(slot, o, e, t):
            value = masked(fold4(t, 0, 1, 2, 3), o, 48, mask48)
            wins_b.add(slot, value, masked(fold4(t, 4, 4, 4, 4), o, 48, mask_low))
            if second:
                to, of, some = own_part(o, e, 48)
                if some:
                    own_ref[5, to, :] = turn(value, -blk)[of]
            if e == n_in - 32:
                wins_b.end(slot)

        def emit_b(slot, o, e, t):
            value = fold4(t, 0, 1, 2, 3) + smooth(0, o + 32, e + 32)
            if not second:
                value = right_nat[o // 32, :, :, :].reshape(32, LANES) - value if e - o == 32 else (
                    right_nat[o // 32, o % 32 // 8 : (o % 32 + e - o) // 8].reshape(e - o, LANES) - value
                )
            value = masked(value, o, 32, mask32)
            state_ref[1, o:e, :] = value
            wins_c.add(slot, value)
            if e == n_in - 64:
                wins_c.end(slot)
                if second:
                    products(step["alpha0"])

        def emit_c(slot, o, e, t):
            blocks = [masked(fold4(t, k, k, k, k), o, 16, masks16[k]) for k in range(3)]
            wins_d.add(slot, blocks)
            if second:
                to, of, some = own_part(o, e, 16)
                if some:
                    value = quarters(*(blocks[k][of] for k in (0, 1, 2, 2)))
                    value = jnp.where(own16, own_ref[5, to, :] - step["alpha0"] * value, 0.0)
                    dots[8] += row_sum(value * value)
            if e == n_in - 96:
                wins_d.end(slot)

        pipeline_of = [
            Stage(0, 5, n_in, 0, emit_a, Feed(buf)),
            Stage(1, 4, n_in - 32, 3, emit_b, before=late_wait if second else right_natural),
            Stage(0, 3, n_in - 64, 6, emit_c),
        ]
        return pipeline_of

    def products(alpha0):
        for o in range(0, cols, 32):
            e = o + 32
            r0 = own_ref[1, o:e, :]
            w1 = jnp.where(own32, state_ref[0, 64 + o : 64 + e, :], 0.0)
            w2 = jnp.where(own32, state_ref[1, 32 + o : 32 + e, :], 0.0)
            bend = smooth(0, 64 + o, 64 + e) - alpha0 * smooth(1, 32 + o, 32 + e)
            r1, q = r0 - alpha0 * w1, w1 - alpha0 * w2
            for k, x in ((2, w1), (3, w2), (4, q), (6, r1)):
                own_ref[k, o:e, :] = x
            for k, x in enumerate((r1 * r1, r1 * q, r1 * w1, w1 * w1, q * q, q * w1, q * w2, w1 * w2, q * bend)):
                dots[k] += row_sum(x)

    rounds = greetings(n_row, n_col)
    receive(first_pack, 0)
    if rounds:
        greet(known_sem.at[0], rounds[0])
    def emit_d(slot, o, e, t):
        r0 = jnp.where(own32, state_ref[1, o + 32 : e + 32, :], 0.0)
        w1 = jnp.where(own32, fold4(t, 0, 0, 1, 1) + smooth(1, o + 32, e + 32), 0.0)
        repack(second_pack, edge2 + o // 16, w1)
        own_ref[1, o:e, :] = r0
        own_ref[0, o:e, :] = state_ref[0, 64 + o : 64 + e, :]
        first_sums[0] += row_sum(r0 * r0)
        first_sums[1] += row_sum(r0 * w1)

    pipeline(three_stages(first_pack, False) + [Stage(1, 2, n_in - 96, 9, emit_d)])
    send(second_pack, 2)
    for k, offsets in enumerate(rounds):
        pl.semaphore_wait(known_sem.at[k], heard(offsets))
        if k + 1 < len(rounds):
            greet(known_sem.at[k + 1], rounds[k + 1])

    def fold(x, down_to):
        k = LANES // 2
        while k >= down_to:
            x = x + turn(x, k)
            k //= 2
        return x

    spread(0, jnp.where(lane1 < 64, fold(first_sums[0], 64), fold(first_sums[1], 64)))
    finish(first_pack, 0)
    each_right(lambda c: c.wait_send(), 1)

    receive(second_pack, 2)
    pipeline(three_stages(second_pack, True))
    m0, m1, alpha0 = step["m0"], step["m1"], step["alpha0"]
    line = fold(dots[8], 64)
    for k in range(8):
        line = jnp.where(jnp.logical_and(lane1 >= 8 * k, lane1 < 8 * k + 8), fold(dots[k], 8), line)
    spread(1, line)
    finish(second_pack, 2)
    all_red(0).wait_send()

    def emit_h(slot, o, e, t):
        w3 = jnp.where(own32, fold4(t, 0, 0, 1, 1) + smooth(1, o + 32, e + 32), 0.0)
        own_ref[5, o:e, :] = own_ref[3, o:e, :] - alpha0 * w3

    pipeline([Stage(1, 2, n_in - 96, 9, emit_h)])

    groups = [(8 * k, 8 * k + 8) for k in range(8)] + [(64, 128)]
    rr1, r1q, r1w, ww, qq, qw, qw2, ww2, qaq = gather(1, groups)
    beta0 = rr1 / m0
    alpha1 = rr1 / (r1q + beta0 * (2.0 * r1w + beta0 * m1))
    both = alpha1 * beta0
    rr2 = rr1 - 2.0 * alpha1 * (r1q + beta0 * r1w) + alpha1 * alpha1 * (
        qq + beta0 * (2.0 * qw + beta0 * ww)
    )
    beta1 = rr2 / rr1
    r2ar2 = (
        r1q + alpha1 * alpha1 * qaq + both * both * ww2
        - 2.0 * alpha1 * qq - 2.0 * both * qw + 2.0 * alpha1 * both * qw2
    )
    alpha2 = rr2 / (r2ar2 - beta1 * rr2 / alpha1)
    t_r0 = alpha0 + both + alpha2 * beta1 * beta0
    t_r1 = alpha1 + alpha2 * (1.0 + beta1)
    t_q, t_w1 = -alpha2 * alpha1, -alpha2 * both
    s_q, s_w1 = -alpha1 - alpha2 * (1.0 + beta1), -both - alpha2 * beta1 * beta0
    s_aq, s_w2 = alpha2 * alpha1, alpha2 * both
    for k in range(0, cols, LANES):
        r1, w1, w2, q, aq, r0 = (own_ref[i, k : k + LANES, :] for i in (6, 2, 3, 4, 5, 1))
        x0 = own_ref[0, k : k + LANES, :]
        template = x0 + t_r0 * r0 + t_r1 * r1 + t_q * q + t_w1 * w1
        residual = r1 + s_q * q + s_w1 * w1 + s_aq * aq + s_w2 * w2
        template_ref[:, k : k + LANES] = template.T[blk : blk + rows]
        residual_ref[:, k : k + LANES] = residual.T[blk : blk + rows]
    all_red(1).wait_send()


def on_device(n_row, n_col, right_side, initial_guess, kernel):
    rows, cols = right_side.shape
    count = n_row * n_col
    shape = pltpu.VMEM((rows, cols), jnp.float32)
    f32, bf16 = jnp.float32, jnp.bfloat16
    tall = cols + 2 * rows
    packs = [pltpu.VMEM((3, cols // 16 + 2 * (rows // 16), 8, LANES), f32) for _ in range(2)]
    packs.insert(1, pltpu.VMEM((6, cols // 32 + 2, 8, LANES), f32))
    return pl.pallas_call(
        functools.partial(body, n_row, n_col),
        out_shape=(shape, shape),
        in_specs=[pl.BlockSpec(memory_space=pl.ANY)] * 3,
        out_specs=[pl.BlockSpec(memory_space=pltpu.VMEM)] * 2,
        scratch_shapes=[
            pltpu.VMEM((rows, cols), f32),
            pltpu.VMEM((rows, cols), f32),
            pltpu.VMEM(kernel.shape, f32),
            *packs,
            pltpu.VMEM((2, LANES, LANES), f32),
            pltpu.VMEM((2, 2, 2 * LANES, 2 * LANES), bf16),
            pltpu.VMEM((2, 5, tall, LANES), bf16),
            pltpu.VMEM((2, 5, tall, LANES), bf16),
            pltpu.VMEM((2, 2, 5, tall, LANES), f32),
            pltpu.VMEM((2, 5, tall, LANES), f32),
            pltpu.VMEM((2, tall, LANES), f32),
            pltpu.VMEM((cols // 32 + 2, 4, 8, LANES), f32),
            pltpu.VMEM((7, cols, LANES), f32),
            pltpu.VMEM((2, count, 1, LANES), f32),
            pltpu.SemaphoreType.DMA((3,)),
            pltpu.SemaphoreType.DMA((3, len(DIRECTIONS))),
            pltpu.SemaphoreType.DMA((3, len(DIRECTIONS))),
            pltpu.SemaphoreType.DMA((2,)),
            pltpu.SemaphoreType.DMA((2,)),
            pltpu.SemaphoreType.REGULAR((len(greetings(n_row, n_col)),)),
        ],
        compiler_params=pltpu.CompilerParams(collective_id=0, has_side_effects=True),
    )(right_side, initial_guess, kernel)


def solution(mesh):
    placed = (P("row", "col"), P("row", "col"), P())
    return jax.shard_map(
        functools.partial(on_device, mesh.shape["row"], mesh.shape["col"]),
        mesh=mesh,
        in_specs=placed,
        out_specs=(P("row", "col"), P("row", "col")),
        check_vma=False,
    )
```

time: 51.5 us -> 28.1 us (0.55)
  Pallas kernels: 48.5 us -> 26 us
  local copies, waits for them, and re-layouts: 2.14 us -> 1.26 us
    pallas_call x1, Pallas kernels: 48.5 us -> 26 us  [on_device(): pl.pallas_call(functools.partial(body, n_row, n_col), out_shape=(shape, s...]
    unnamed x4 -> x2, local copies, waits for them, and re-layouts: 2.14 us -> 1.26 us
where the time goes in v3:
time: 28.1 us; the launch traced here: 27.9 us
  Pallas kernels  26 us (93%)
  local copies, waits for them, and re-layouts  1.26 us (4%)
  between operations  0.64 us (2%)
    pallas_call x1, Pallas kernels, on_device(): pl.pallas_call(functools.partial(body, n_row, n_col), out_shape=(shape, s...  26 us
    unnamed x2, local copies, waits for them, and re-layouts  1.26 us

profile of v3, /device:TPU:0, one launch (start us, length us, event | category | flops | bytes accessed | tf_op | source)
XLA Modules:
  0.0 27.9 jit_solution(11280597791313683445)
XLA Ops:
  0.6 26.0 %shard_map.50 = (f32[64,256]{1,0:T(8,128)S(1)}, f32[64,256]{1,0:T(8,128)S(1)}) custom-call(f32[64,256]{1,0:T(8,128)} %refs_0_.1, f32[64,256]{1,0:T(8,128)} %refs_1_.1, f32[31,31]{1,0:T(8,128)} %refs_2_.1), custom_call_target="tpu_custom_call" | custom-call | tf_op jit(solution)/shard_map/pallas_call | solution.py:737
  26.6 0.6 %copy.7 = f32[64,256]{1,0:T(8,128)} copy(f32[64,256]{1,0:T(8,128)S(1)} %get-tuple-element.2) | data formatting | bytes 131072
  27.3 0.6 %copy.8 = f32[64,256]{1,0:T(8,128)} copy(f32[64,256]{1,0:T(8,128)S(1)} %get-tuple-element.3) | data formatting | bytes 131072

commit v4 on v3

--- a/solution.py
+++ b/solution.py
@@ -73,7 +73,7 @@
 
 def run(
     n_row, n_col, accs,
-    right_hbm, guess_hbm, kernel_hbm, template_ref, residual_ref,
+    right_hbm, guess_hbm, kernel_hbm, template_ref, residual_ref, shared_ref,
     right_ref, guess_ref, kernel_ref, first_pack, right_pack, second_pack,
     lines_ref, table, high_ref, low_ref, wide, partial_ref,
     state_ref, right_nat, own_ref, red, load_sem, send_sem, recv_sem, red_send, red_recv, known_sem,
@@ -385,13 +385,13 @@
         return out
 
     class Windows:
-        def __init__(self, n):
-            self.n, self.kept, self.at = n, None, 0
+        def __init__(self, n, blocks=False):
+            self.n, self.blocks, self.kept, self.at = n, blocks, None, 0
 
         def make(self, slot, parts):
             size = parts[0].shape[0] - 16
-            if self.n == 2:
-                for k in range(2):
+            if self.blocks:
+                for k in range(self.n):
                     a, b = parts[k], parts[k + 1]
                     win = quarters(a[0:size], b[0:size], a[8 : size + 8], b[8 : size + 8])
                     put_window(slot, k, self.at, win)
@@ -418,7 +418,7 @@
             self.at += size
 
         def add(self, slot, value, extra=None):
-            if self.n == 2:
+            if self.blocks:
                 parts = value
             else:
                 parts = [value, turn(value, blk), turn(value, 2 * blk), turn(value, 3 * blk), extra]
@@ -443,12 +443,44 @@
 
     def repack(buf, group, value):
         n = value.shape[0] // 16
-        down, up = (turn(value, by).reshape(n, 2, 8, LANES) for by in (-blk, blk))
-        buf[1, group : group + n] = jnp.where(low_half(down[:, 0]), down[:, 0], up[:, 1])
+        down, up = (turn(value, by).reshape(n, 2, 8, LANES) for by in (-16, 48))
+        q = lanes_of((n, 8, LANES))
+        lower = jnp.where(q < 16, up[:, 0], down[:, 0])
+        upper = jnp.where(q < 80, down[:, 1], up[:, 1])
+        buf[1, group : group + n] = jnp.where(q < 64, lower, upper)
+
+    def swap(x):
+        odd = lax.rem(lanes_of(x.shape) // blk, 2) == 1
+        return jnp.where(odd, turn(x, blk), turn(x, -blk))
+
+    class RolledFeed:
+        def __init__(self, buf, first):
+            self.buf, self.first, self.at = buf, first, 0
+
+        def __call__(self, slot, upto):
+            upto = min(upto, (self.buf.shape[1] - 2 * self.first) * 16)
+            while self.at < upto:
+                size = min(2, (upto - self.at) // 16)
+                self.two(slot, self.first + self.at // 16, size)
+                self.at += size * 16
+
+        def two(self, slot, first, size):
+            up, mid, down = (expand(self.buf, k, first, size) for k in range(3))
+            at = self.at
+            q = lax.rem(lanes_of(mid.shape), 2 * blk)
+            second = jnp.where(q < 16, up, mid)
+            fourth = jnp.where(q < 16, mid, down)
+            start = swap(jnp.where(q < 16, up, jnp.where(q < blk, mid, up)))
+            third = swap(jnp.where(jnp.logical_and(q >= 16, q < blk), down, mid))
+            for k, w in enumerate((start, second, third, fourth)):
+                put_window(slot, k, at, w)
+            state_ref[0, at : at + size * 16, :] = jnp.where(
+                low_half(mid), second, turn(fourth, 2 * blk)
+            )
 
     class Feed:
-        def __init__(self, buf):
-            self.buf, self.at = buf, 0
+        def __init__(self, buf, rolled):
+            self.buf, self.rolled, self.at = buf, rolled, 0
 
         def __call__(self, slot, upto):
             upto = min(upto, self.buf.shape[1] * 16)
@@ -458,6 +490,9 @@
         def two(self, slot, first, size):
             up, mid, down = (expand(self.buf, s, first, size) for s in range(3))
             at = self.at
+            if self.rolled:
+                far = lax.rem(lanes_of(mid.shape), 2 * blk) >= 48
+                up, mid, down = (jnp.where(far, turn(x, 48), turn(x, -16)) for x in (up, mid, down))
             odd = lax.rem(lanes_of(mid.shape), 2 * blk) >= blk
             upper = jnp.where(odd, turn(mid, blk), turn(up, -blk))
             lower = jnp.where(odd, turn(down, blk), turn(mid, -blk))
@@ -572,7 +607,7 @@
     loads[2].wait()
     build_tables()
 
-    mask48, mask32 = (row_mask(lane1 - k) for k in (48, 32))
+    mask48, mask32, mask16 = (row_mask(lane1 - k) for k in (48, 32, 16))
     mask_low = row_mask(rows + 16 + 0 * lane1)
     masks16 = [row_mask(blk * k - 16 + lax.rem(lane1, blk)) for k in range(3)]
     own32 = jnp.logical_and(lane1 >= 32, lane1 < 32 + rows)
@@ -592,15 +627,11 @@
         step["alpha0"] = step["m0"] / step["m1"]
 
     def three_stages(buf, second):
-        wins_b, wins_c, wins_d = Windows(4), Windows(3), Windows(2)
+        wins_b, wins_c, wins_d = Windows(4), Windows(3), Windows(2, True)
 
         def emit_a(slot, o, e, t):
             value = masked(fold4(t, 0, 1, 2, 3), o, 48, mask48)
             wins_b.add(slot, value, masked(fold4(t, 4, 4, 4, 4), o, 48, mask_low))
-            if second:
-                to, of, some = own_part(o, e, 48)
-                if some:
-                    own_ref[5, to, :] = turn(value, -blk)[of]
             if e == n_in - 32:
                 wins_b.end(slot)
 
@@ -615,35 +646,58 @@
             wins_c.add(slot, value)
             if e == n_in - 64:
                 wins_c.end(slot)
-                if second:
-                    products(step["alpha0"])
 
         def emit_c(slot, o, e, t):
             blocks = [masked(fold4(t, k, k, k, k), o, 16, masks16[k]) for k in range(3)]
             wins_d.add(slot, blocks)
-            if second:
-                to, of, some = own_part(o, e, 16)
-                if some:
-                    value = quarters(*(blocks[k][of] for k in (0, 1, 2, 2)))
-                    value = jnp.where(own16, own_ref[5, to, :] - step["alpha0"] * value, 0.0)
-                    dots[8] += row_sum(value * value)
             if e == n_in - 96:
                 wins_d.end(slot)
 
         pipeline_of = [
-            Stage(0, 5, n_in, 0, emit_a, Feed(buf)),
-            Stage(1, 4, n_in - 32, 3, emit_b, before=late_wait if second else right_natural),
+            Stage(0, 5, n_in, 0, emit_a, Feed(buf, second)),
+            Stage(1, 4, n_in - 32, 3, emit_b, before=None if second else right_natural),
             Stage(0, 3, n_in - 64, 6, emit_c),
         ]
         return pipeline_of
+
+    def early_stages(buf):
+        wins_f, wins_g = Windows(3), Windows(2)
+        n_two = n_in - 32
+
+        def emit_e(slot, o, e, t):
+            value = masked(fold4(t, 0, 1, 2, 3), o, 32, mask32)
+            to, of, some = own_part(o, e, 32)
+            if some:
+                own_ref[5, to, :] = value[of]
+            wins_f.add(slot, value)
+            if e == n_two - 32:
+                wins_f.end(slot)
+
+        def emit_f(slot, o, e, t):
+            value = masked(fold4(t, 0, 1, 2, 2) + smooth(0, o + 32, e + 32), o, 16, mask16)
+            state_ref[1, o:e, :] = value
+            wins_g.add(slot, value)
+            if e == n_two - 64:
+                wins_g.end(slot)
+                products(step["alpha0"])
+
+        def emit_g(slot, o, e, t):
+            value = jnp.where(own32, own_ref[5, o:e, :] - step["alpha0"] * fold4(t, 0, 0, 1, 1), 0.0)
+            dots[8] += row_sum(value * value)
+
+        return [
+            Stage(0, 4, n_two, 2, emit_e, RolledFeed(buf, 1)),
+            Stage(1, 3, n_two - 32, 5, emit_f, before=late_wait),
+            Stage(0, 2, n_two - 64, 8, emit_g),
+        ]
 
     def products(alpha0):
         for o in range(0, cols, 32):
             e = o + 32
             r0 = own_ref[1, o:e, :]
-            w1 = jnp.where(own32, state_ref[0, 64 + o : 64 + e, :], 0.0)
-            w2 = jnp.where(own32, state_ref[1, 32 + o : 32 + e, :], 0.0)
-            bend = smooth(0, 64 + o, 64 + e) - alpha0 * smooth(1, 32 + o, 32 + e)
+            w1 = jnp.where(own16, state_ref[0, 48 + o : 48 + e, :], 0.0)
+            w2 = jnp.where(own16, state_ref[1, 16 + o : 16 + e, :], 0.0)
+            bend = smooth(0, 48 + o, 48 + e) - alpha0 * smooth(1, 16 + o, 16 + e)
             r1, q = r0 - alpha0 * w1, w1 - alpha0 * w2
             for k, x in ((2, w1), (3, w2), (4, q), (6, r1)):
                 own_ref[k, o:e, :] = x
@@ -658,8 +712,6 @@
         r0 = jnp.where(own32, state_ref[1, o + 32 : e + 32, :], 0.0)
         w1 = jnp.where(own32, fold4(t, 0, 0, 1, 1) + smooth(1, o + 32, e + 32), 0.0)
         repack(second_pack, edge2 + o // 16, w1)
-        own_ref[1, o:e, :] = r0
-        own_ref[0, o:e, :] = state_ref[0, 64 + o : 64 + e, :]
         first_sums[0] += row_sum(r0 * r0)
         first_sums[1] += row_sum(r0 * w1)
 
@@ -681,8 +733,10 @@
     finish(first_pack, 0)
     each_right(lambda c: c.wait_send(), 1)
 
+    own_ref[0] = jnp.where(own16, turn(state_ref[0, 64 : 64 + cols, :], -16), 0.0)
+    own_ref[1] = jnp.where(own16, turn(state_ref[1, 32 : 32 + cols, :], -16), 0.0)
     receive(second_pack, 2)
-    pipeline(three_stages(second_pack, True))
+    pipeline(early_stages(second_pack))
     m0, m1, alpha0 = step["m0"], step["m1"], step["alpha0"]
     line = fold(dots[8], 64)
     for k in range(8):
@@ -693,9 +747,13 @@
 
     def emit_h(slot, o, e, t):
         w3 = jnp.where(own32, fold4(t, 0, 0, 1, 1) + smooth(1, o + 32, e + 32), 0.0)
+        w3 = turn(w3, -16)
         own_ref[5, o:e, :] = own_ref[3, o:e, :] - alpha0 * w3
 
-    pipeline([Stage(1, 2, n_in - 96, 9, emit_h)])
+    pipeline(three_stages(second_pack, True) + [Stage(1, 2, n_in - 96, 9, emit_h)])
+
+    for k in range(0, cols, LANES):
+        shared_ref[:, k : k + LANES] = own_ref[6, k : k + LANES, :].T[16 : 16 + rows]
 
     groups = [(8 * k, 8 * k + 8) for k in range(8)] + [(64, 128)]
     rr1, r1q, r1w, ww, qq, qw, qw2, ww2, qaq = gather(1, groups)
@@ -719,10 +777,10 @@
     for k in range(0, cols, LANES):
         r1, w1, w2, q, aq, r0 = (own_ref[i, k : k + LANES, :] for i in (6, 2, 3, 4, 5, 1))
         x0 = own_ref[0, k : k + LANES, :]
-        template = x0 + t_r0 * r0 + t_r1 * r1 + t_q * q + t_w1 * w1
-        residual = r1 + s_q * q + s_w1 * w1 + s_aq * aq + s_w2 * w2
-        template_ref[:, k : k + LANES] = template.T[blk : blk + rows]
-        residual_ref[:, k : k + LANES] = residual.T[blk : blk + rows]
+        template = x0 + t_r0 * r0 + (t_r1 - 1.0) * r1 + t_q * q + t_w1 * w1
+        residual = s_q * q + s_w1 * w1 + s_aq * aq + s_w2 * w2
+        template_ref[:, k : k + LANES] = template.T[16 : 16 + rows]
+        residual_ref[:, k : k + LANES] = residual.T[16 : 16 + rows]
     all_red(1).wait_send()
 
 
@@ -734,11 +792,11 @@
     tall = cols + 2 * rows
     packs = [pltpu.VMEM((3, cols // 16 + 2 * (rows // 16), 8, LANES), f32) for _ in range(2)]
     packs.insert(1, pltpu.VMEM((6, cols // 32 + 2, 8, LANES), f32))
-    return pl.pallas_call(
+    template, residual, shared = pl.pallas_call(
         functools.partial(body, n_row, n_col),
-        out_shape=(shape, shape),
+        out_shape=(shape,) * 3,
         in_specs=[pl.BlockSpec(memory_space=pl.ANY)] * 3,
-        out_specs=[pl.BlockSpec(memory_space=pltpu.VMEM)] * 2,
+        out_specs=[pl.BlockSpec(memory_space=pltpu.VMEM)] * 3,
         scratch_shapes=[
             pltpu.VMEM((rows, cols), f32),
             pltpu.VMEM((rows, cols), f32),
@@ -763,6 +821,7 @@
         ],
         compiler_params=pltpu.CompilerParams(collective_id=0, has_side_effects=True),
     )(right_side, initial_guess, kernel)
+    return template + shared, residual + shared
 
 
 def solution(mesh):

time: 28.1 us -> 26.8 us (0.954)
  local copies, waits for them, and re-layouts: 1.26 us -> 0 us
  other arithmetic: 0 us -> 0.67 us
  Pallas kernels: 26 us -> 25.4 us
    unnamed x2 -> x0, local copies, waits for them, and re-layouts: 1.26 us -> none
    add x0 -> x1, other arithmetic: none -> 0.67 us  [on_device(): return (template + shared, residual + shared)]
    pallas_call x1, Pallas kernels: 26 us -> 25.4 us  [on_device(): pl.pallas_call(functools.partial(body, n_row, n_col), out_shape=(shape,)...]
where the time goes in v4:
time: 26.8 us; the launch traced here: 26.7 us
  Pallas kernels  25.4 us (95%)
  other arithmetic  0.67 us (2%)
  between operations  0.64 us (2%)
    pallas_call x1, Pallas kernels, on_device(): pl.pallas_call(functools.partial(body, n_row, n_col), out_shape=(shape,)...  25.4 us
    add x1, other arithmetic, on_device(): return (template + shared, residual + shared)  0.67 us

profile of v4, /device:TPU:0, one launch (start us, length us, event | category | flops | bytes accessed | tf_op | source)
XLA Modules:
  0.0 26.7 jit_solution(14537957800853457407)
XLA Ops:
  0.6 25.4 %shard_map.50 = (f32[64,256]{1,0:T(8,128)S(1)}, f32[64,256]{1,0:T(8,128)S(1)}, f32[64,256]{1,0:T(8,128)S(1)}) custom-call(f32[64,256]{1,0:T(8,128)} %refs_0_.1, f32[64,256]{1,0:T(8,128)} %refs_1_.1, f32[31,31]{1,0:T(8,128)} %refs_2_.1), custom_call_target="tpu_custom_call" | custom-call | tf_op jit(solution)/shard_map/pallas_call | solution.py:795
  26.0 0.7 %fusion = (f32[64,256]{1,0:T(8,128)}, f32[64,256]{1,0:T(8,128)}) fusion(f32[64,256]{1,0:T(8,128)S(1)} %get-tuple-element.7, f32[64,256]{1,0:T(8,128)S(1)} %get-tuple-element.6, f32[64,256]{1,0:T(8,128)S(1)} %get-tuple-element.5), kind=kLoop, calls=%fused_computation | loop fusion | flops 32768 | bytes 327680 | tf_op jit(solution)/shard_map/add | solution.py:824

commit v5 on v4

--- a/solution.py
+++ b/solution.py
@@ -14,7 +14,7 @@
 STEPS = (8, 15, 20)
 SUMS = 9
 MESH = pl.DeviceIdType.MESH
-DIRECTIONS = ((-1, 0), (1, 0), (-1, -1), (-1, 1), (1, -1), (1, 1), (0, -1), (0, 1))
+DIRECTIONS = ((-1, -1), (-1, 1), (1, -1), (1, 1), (-1, 0), (1, 0), (0, -1), (0, 1))
 
 
 NEAR = tuple((a, b) for a in (-1, 0, 1) for b in (-1, 0, 1) if (a, b) != (0, 0))
@@ -76,7 +76,7 @@
     right_hbm, guess_hbm, kernel_hbm, template_ref, residual_ref, shared_ref,
     right_ref, guess_ref, kernel_ref, first_pack, right_pack, second_pack,
     lines_ref, table, high_ref, low_ref, wide, partial_ref,
-    state_ref, right_nat, own_ref, red, load_sem, send_sem, recv_sem, red_send, red_recv, known_sem,
+    state_ref, right_nat, own_ref, upright_ref, red, load_sem, send_sem, recv_sem, red_send, red_recv, known_sem,
 ):
     rows, cols = right_ref.shape
     row, col = lax.axis_index("row"), lax.axis_index("col")
@@ -501,8 +501,15 @@
             state_ref[0, at : at + size * 16, :] = jnp.where(low_half(mid), upper, turn(lower, 2 * blk))
             self.at += size * 16
 
-    def row_sum(x):
-        return jnp.sum(x, axis=0, keepdims=True)
+    def tile_sum(x):
+        return jnp.sum(x.reshape(-1, 8, LANES), axis=0)
+
+    def collect(totals):
+        line = jnp.zeros((1, LANES), jnp.float32)
+        for k, x in enumerate(totals):
+            x = jnp.sum(jnp.sum(x, axis=0, keepdims=True), axis=1, keepdims=True)
+            line = jnp.where(lane1 == k, x, line)
+        return line
 
     def red_copy(turn_no, place):
         return pltpu.make_async_remote_copy(
@@ -533,14 +540,11 @@
                 if r or c:
                     red_copy(turn_no, (flipped(row, n_row, r), flipped(col, n_col, c))).start()
 
-    def gather(turn_no, groups):
+    def gather(turn_no, n):
         all_red(turn_no).wait_recv()
         line = jnp.sum(red[turn_no], axis=0)
         return [
-            jnp.sum(
-                jnp.where(jnp.logical_and(lane1 >= a, lane1 < b), line, 0.0), axis=1, keepdims=True
-            )
-            for a, b in groups
+            jnp.sum(jnp.where(lane1 == k, line, 0.0), axis=1, keepdims=True) for k in range(n)
         ]
 
     right_groups = right_pack.shape[1]
@@ -623,7 +627,7 @@
     step = {}
 
     def late_wait():
-        step["m0"], step["m1"] = gather(0, ((0, 64), (64, 128)))
+        step["m0"], step["m1"] = gather(0, 2)
         step["alpha0"] = step["m0"] / step["m1"]
 
     def three_stages(buf, second):
@@ -679,16 +683,17 @@
             wins_g.add(slot, value)
             if e == n_two - 64:
                 wins_g.end(slot)
+
+        def emit_g(slot, o, e, t):
+            if o == 32:
                 products(step["alpha0"])
-
-        def emit_g(slot, o, e, t):
             value = jnp.where(own32, own_ref[5, o:e, :] - step["alpha0"] * fold4(t, 0, 0, 1, 1), 0.0)
-            dots[8] += row_sum(value * value)
+            dots[8] += tile_sum(value * value)
 
         return [
             Stage(0, 4, n_two, 2, emit_e, RolledFeed(buf, 1)),
-            Stage(1, 3, n_two - 32, 5, emit_f, before=late_wait),
-            Stage(0, 2, n_two - 64, 8, emit_g),
+            Stage(1, 3, n_two - 32, 5, emit_f),
+            Stage(0, 2, n_two - 64, 8, emit_g, before=late_wait),
         ]
 
     def products(alpha0):
@@ -702,7 +707,7 @@
             for k, x in ((2, w1), (3, w2), (4, q), (6, r1)):
                 own_ref[k, o:e, :] = x
             for k, x in enumerate((r1 * r1, r1 * q, r1 * w1, w1 * w1, q * q, q * w1, q * w2, w1 * w2, q * bend)):
-                dots[k] += row_sum(x)
+                dots[k] += tile_sum(x)
 
     rounds = greetings(n_row, n_col)
     receive(first_pack, 0)
@@ -712,8 +717,8 @@
         r0 = jnp.where(own32, state_ref[1, o + 32 : e + 32, :], 0.0)
         w1 = jnp.where(own32, fold4(t, 0, 0, 1, 1) + smooth(1, o + 32, e + 32), 0.0)
         repack(second_pack, edge2 + o // 16, w1)
-        first_sums[0] += row_sum(r0 * r0)
-        first_sums[1] += row_sum(r0 * w1)
+        first_sums[0] += tile_sum(r0 * r0)
+        first_sums[1] += tile_sum(r0 * w1)
 
     pipeline(three_stages(first_pack, False) + [Stage(1, 2, n_in - 96, 9, emit_d)])
     send(second_pack, 2)
@@ -722,26 +727,15 @@
         if k + 1 < len(rounds):
             greet(known_sem.at[k + 1], rounds[k + 1])
 
-    def fold(x, down_to):
-        k = LANES // 2
-        while k >= down_to:
-            x = x + turn(x, k)
-            k //= 2
-        return x
-
-    spread(0, jnp.where(lane1 < 64, fold(first_sums[0], 64), fold(first_sums[1], 64)))
+    spread(0, collect(first_sums))
     finish(first_pack, 0)
     each_right(lambda c: c.wait_send(), 1)
 
-    own_ref[0] = jnp.where(own16, turn(state_ref[0, 64 : 64 + cols, :], -16), 0.0)
     own_ref[1] = jnp.where(own16, turn(state_ref[1, 32 : 32 + cols, :], -16), 0.0)
     receive(second_pack, 2)
     pipeline(early_stages(second_pack))
     m0, m1, alpha0 = step["m0"], step["m1"], step["alpha0"]
-    line = fold(dots[8], 64)
-    for k in range(8):
-        line = jnp.where(jnp.logical_and(lane1 >= 8 * k, lane1 < 8 * k + 8), fold(dots[k], 8), line)
-    spread(1, line)
+    spread(1, collect(dots))
     finish(second_pack, 2)
     all_red(0).wait_send()
 
@@ -752,11 +746,16 @@
 
     pipeline(three_stages(second_pack, True) + [Stage(1, 2, n_in - 96, 9, emit_h)])
 
-    for k in range(0, cols, LANES):
-        shared_ref[:, k : k + LANES] = own_ref[6, k : k + LANES, :].T[16 : 16 + rows]
-
-    groups = [(8 * k, 8 * k + 8) for k in range(8)] + [(64, 128)]
-    rr1, r1q, r1w, ww, qq, qw, qw2, ww2, qaq = gather(1, groups)
+    def upright(k):
+        return jnp.concatenate(
+            [own_ref[k, j : j + LANES, :].T[16 : 16 + rows] for j in range(0, cols, LANES)], axis=1
+        )
+
+    shared_ref[...] = upright(6)
+    for at, k in enumerate((1, 2, 3, 4, 5)):
+        upright_ref[at] = upright(k)
+
+    rr1, r1q, r1w, ww, qq, qw, qw2, ww2, qaq = gather(1, SUMS)
     beta0 = rr1 / m0
     alpha1 = rr1 / (r1q + beta0 * (2.0 * r1w + beta0 * m1))
     both = alpha1 * beta0
@@ -774,13 +773,9 @@
     t_q, t_w1 = -alpha2 * alpha1, -alpha2 * both
     s_q, s_w1 = -alpha1 - alpha2 * (1.0 + beta1), -both - alpha2 * beta1 * beta0
     s_aq, s_w2 = alpha2 * alpha1, alpha2 * both
-    for k in range(0, cols, LANES):
-        r1, w1, w2, q, aq, r0 = (own_ref[i, k : k + LANES, :] for i in (6, 2, 3, 4, 5, 1))
-        x0 = own_ref[0, k : k + LANES, :]
-        template = x0 + t_r0 * r0 + (t_r1 - 1.0) * r1 + t_q * q + t_w1 * w1
-        residual = s_q * q + s_w1 * w1 + s_aq * aq + s_w2 * w2
-        template_ref[:, k : k + LANES] = template.T[16 : 16 + rows]
-        residual_ref[:, k : k + LANES] = residual.T[16 : 16 + rows]
+    r0, w1, w2, q, aq = (upright_ref[k] for k in range(5))
+    template_ref[...] = guess_ref[...] + t_r0 * r0 + (t_r1 - 1.0) * shared_ref[...] + t_q * q + t_w1 * w1
+    residual_ref[...] = s_q * q + s_w1 * w1 + s_aq * aq + s_w2 * w2
     all_red(1).wait_send()
 
 
@@ -811,6 +806,7 @@
             pltpu.VMEM((2, tall, LANES), f32),
             pltpu.VMEM((cols // 32 + 2, 4, 8, LANES), f32),
             pltpu.VMEM((7, cols, LANES), f32),
+            pltpu.VMEM((5, rows, cols), f32),
             pltpu.VMEM((2, count, 1, LANES), f32),
             pltpu.SemaphoreType.DMA((3,)),
             pltpu.SemaphoreType.DMA((3, len(DIRECTIONS))),

time: 26.8 us -> 25.8 us (0.963)
  Pallas kernels: 25.4 us -> 24.3 us
    pallas_call x1, Pallas kernels: 25.4 us -> 24.3 us  [on_device(): pl.pallas_call(functools.partial(body, n_row, n_col), out_shape=(shape,)...]
where the time goes in v5:
time: 25.8 us; the launch traced here: 25.6 us
  Pallas kernels  24.3 us (94%)
  other arithmetic  0.67 us (3%)
  between operations  0.64 us (2%)
    pallas_call x1, Pallas kernels, on_device(): pl.pallas_call(functools.partial(body, n_row, n_col), out_shape=(shape,)...  24.3 us
    add x1, other arithmetic, on_device(): return (template + shared, residual + shared)  0.67 us

profile of v5, /device:TPU:0, one launch (start us, length us, event | category | flops | bytes accessed | tf_op | source)
XLA Modules:
  0.0 25.6 jit_solution(18166119682774058260)
XLA Ops:
  0.6 24.3 %shard_map.50 = (f32[64,256]{1,0:T(8,128)S(1)}, f32[64,256]{1,0:T(8,128)S(1)}, f32[64,256]{1,0:T(8,128)S(1)}) custom-call(f32[64,256]{1,0:T(8,128)} %refs_0_.1, f32[64,256]{1,0:T(8,128)} %refs_1_.1, f32[31,31]{1,0:T(8,128)} %refs_2_.1), custom_call_target="tpu_custom_call" | custom-call | tf_op jit(solution)/shard_map/pallas_call | solution.py:790
  24.9 0.7 %fusion = (f32[64,256]{1,0:T(8,128)}, f32[64,256]{1,0:T(8,128)}) fusion(f32[64,256]{1,0:T(8,128)S(1)} %get-tuple-element.7, f32[64,256]{1,0:T(8,128)S(1)} %get-tuple-element.6, f32[64,256]{1,0:T(8,128)S(1)} %get-tuple-element.5), kind=kLoop, calls=%fused_computation | loop fusion | flops 32768 | bytes 327680 | tf_op jit(solution)/shard_map/add | solution.py:820

commit v6 on v5

--- a/solution.py
+++ b/solution.py
@@ -18,7 +18,7 @@
 
 
 NEAR = tuple((a, b) for a in (-1, 0, 1) for b in (-1, 0, 1) if (a, b) != (0, 0))
-GREET = NEAR + ((0, -4), (0, 4))
+GREET = tuple(sorted(NEAR, key=lambda p: -abs(p[0]) - abs(p[1]))) + ((0, -4), (0, 4))
 
 
 def square(r, c):

time: 25.8 us -> 25.7 us (level)
  no operation moved by 1% of the time
where the time goes in v6:
time: 25.7 us; the launch traced here: 25.6 us
  Pallas kernels  24.3 us (95%)
  other arithmetic  0.67 us (3%)
  between operations  0.64 us (2%)
    pallas_call x1, Pallas kernels, on_device(): pl.pallas_call(functools.partial(body, n_row, n_col), out_shape=(shape,)...  24.3 us
    add x1, other arithmetic, on_device(): return (template + shared, residual + shared)  0.67 us

profile of v6, /device:TPU:0, one launch (start us, length us, event | category | flops | bytes accessed | tf_op | source)
XLA Modules:
  0.0 25.6 jit_solution(12602447442395525503)
XLA Ops:
  0.6 24.3 %shard_map.50 = (f32[64,256]{1,0:T(8,128)S(1)}, f32[64,256]{1,0:T(8,128)S(1)}, f32[64,256]{1,0:T(8,128)S(1)}) custom-call(f32[64,256]{1,0:T(8,128)} %refs_0_.1, f32[64,256]{1,0:T(8,128)} %refs_1_.1, f32[31,31]{1,0:T(8,128)} %refs_2_.1), custom_call_target="tpu_custom_call" | custom-call | tf_op jit(solution)/shard_map/pallas_call | solution.py:790
  24.9 0.7 %fusion = (f32[64,256]{1,0:T(8,128)}, f32[64,256]{1,0:T(8,128)}) fusion(f32[64,256]{1,0:T(8,128)S(1)} %get-tuple-element.7, f32[64,256]{1,0:T(8,128)S(1)} %get-tuple-element.6, f32[64,256]{1,0:T(8,128)S(1)} %get-tuple-element.5), kind=kLoop, calls=%fused_computation | loop fusion | flops 32768 | bytes 327680 | tf_op jit(solution)/shard_map/add | solution.py:820
